TPU v7x, 32 devices: a whole 2x2x4 slice. The times are simulated.
32 devices in a mesh: expert: 8 (over y, x, core), row: 4 (over z).
Axes of the slice: x: 2, y: 2, z: 4, core: 2. Of those that a mesh axis runs over, the one named last changes fastest.
Arguments:
- weights: bfloat16 [8, 7168, 2048], P('expert', 'row'), may hold values from -6 to 6
- left_bits: int32 [8, 7168], P('expert', 'row'), may hold values from 0 to 1
- right_bits: int32 [8, 2048], P('expert'), may hold values from 0 to 1
- groups: int32 [8, 2048], P('expert'), may hold values from 0 to 15, never falling along the last dimension, each value on 1 to 256 neighbouring positions
Outputs:
- scaled: bfloat16 [8, 7168, 2048], P('expert', 'row')
- block_error: float32 [8, 7168, 256], P('expert', 'row')
- scales: float32 [8, 16], P('expert')
- expert_error: float32 [8], P('expert')
- total_error: float32 [], replicated
Inputs may be any that keep to these rules, and one draw needn't show every extreme that they name: Along each expert's 2048 columns the group number never falls; each of the 16 groups holds 1 to 256 columns.
All inputs are finite; a program needn't handle non-finite values.
Results may differ from a plain program's by a relative error of at most 0.0091.
Values may be sent and summed in bfloat16 or wider, within the bound.
A program may use at most 192 MiB of HBM per device.

v0:
```python
import functools
import math

import jax
import jax.numpy as jnp
from jax import lax
from jax.experimental import pallas as pl
from jax.experimental.pallas import tpu as pltpu
from jax.sharding import PartitionSpec as P

HB = 128
SUB = 16
FOLD = HB // SUB
OCT = 8
LANES = 128
GROUPS = 16
BLOCKS = 56
MESH = pl.DeviceIdType.MESH


def signs(common, bits):
    for shift in (4, 2, 1):
        if shift < bits:
            common = common ^ (common >> shift)
    return (1 - 2 * (common & 1)).astype(jnp.float32)


def iota(shape, dim):
    return lax.broadcasted_iota(jnp.int32, shape, dim)


def down(row):
    return jnp.broadcast_to(row, (LANES, LANES)).T


def cosine_block(order):
    first = jnp.arange(order, dtype=jnp.float32)[:, None]
    second = jnp.arange(order, dtype=jnp.float32)[None, :]
    table = math.sqrt(2.0 / order) * jnp.cos(math.pi * (2.0 * second + 1.0) * first / (2.0 * order))
    return jnp.where(first == 0.0, table * math.sqrt(0.5), table)


def build_column(right_ref, h_ref, scale):
    slabs = h_ref.shape[3] // LANES
    half = h_ref.shape[2]
    square = (LANES, LANES)
    octave = [signs((iota(square, 0) & (OCT - 1)) & s, 3) for s in range(OCT)]

    def step(u, _):
        at = pl.ds(pl.multiple_of(u * LANES, LANES), LANES)
        outer = signs(((u * LANES + iota(square, 0)) >> 3) & iota(square, 1), 7)
        for side in range(2):
            bits = right_ref[:, pl.ds(pl.multiple_of(side * half + u * LANES, LANES), LANES)]
            part = outer * down((2 * bits - 1).astype(jnp.float32) * scale)
            for s in range(OCT):
                q, slab = s // slabs, s % slabs
                h_ref[side, q, at, slab * LANES:(slab + 1) * LANES] = (part * octave[s]).astype(jnp.bfloat16)
        return 0

    lax.fori_loop(0, half // LANES, step, 0)


def build_left(left_ref, left):
    def step(j, _):
        bits = left_ref[:, pl.ds(pl.multiple_of(j * HB, HB), HB)]
        left[j] = down((2 * bits - 1).astype(jnp.float32))
        return 0

    lax.fori_loop(0, left.shape[0], step, 0)


def build_row(cosine_ref, m_ref):
    size = m_ref.shape[0]
    spread = (iota((size, BLOCKS), 0) // SUB == iota((size, BLOCKS), 1)).astype(jnp.float32).astype(jnp.bfloat16)
    chunk = size // 7

    def step(u, _):
        at = pl.multiple_of(u * chunk, chunk)
        here = ((at + iota((chunk, BLOCKS), 0)) // SUB == iota((chunk, BLOCKS), 1)).astype(jnp.float32)
        rows = jnp.dot(here.astype(jnp.bfloat16), cosine_ref[...], preferred_element_type=jnp.float32)
        full = lax.dot_general(
            rows.astype(jnp.bfloat16), spread, (((1,), (1,)), ((), ())), preferred_element_type=jnp.float32
        )
        small = signs((iota((chunk, size), 0) & iota((chunk, size), 1)) & (SUB - 1), 4)
        m_ref[pl.ds(at, chunk), :] = (full * small).astype(jnp.bfloat16)
        return 0

    lax.fori_loop(0, 7, step, 0)


def build_order(p_ref):
    half = p_ref.shape[0]

    def step(s, _):
        wanted = iota((LANES, half), 0) * OCT + s
        hit = (wanted == iota((LANES, half), 1)).astype(jnp.float32)
        p_ref[pl.ds(pl.multiple_of(s * LANES, LANES), LANES), :] = hit.astype(jnp.bfloat16)
        return 0

    lax.fori_loop(0, OCT, step, 0)


def fold_rows(parts):
    step = 1
    while step < len(parts):
        mixed = list(parts)
        for k in range(len(parts)):
            if not k & step:
                mixed[k] = parts[k] + parts[k + step]
                mixed[k + step] = parts[k] - parts[k + step]
        parts, step = mixed, 2 * step
    return parts


def kernel(
    peers, experts, x_hbm, left_ref, right_ref, group_ref, cosine_ref,
    scaled_ref, error_ref, scale_ref, mean_ref, total_ref,
    x_ref, left, h_ref, m_ref, p_ref, out1, in1, out2, in2, peaks, turned,
    sum_ref, row_sums, expert_sums,
    send1, recv1, send2, recv2, send3, recv3, send4, recv4, send5, recv5, load_sem,
):
    blocks, _, width = x_ref.shape
    half = width // 2
    lanes = h_ref.shape[3]
    slabs = lanes // LANES
    rows = blocks * SUB
    me = lax.axis_index("row")
    mine = lax.axis_index("expert")
    load = pltpu.make_async_copy(x_hbm, x_ref, load_sem)
    load.start()
    far_first = sorted(range(1, peers), key=lambda d: (abs(d - peers // 2), d))
    others = [lax.rem(me + d, peers) for d in far_first]
    elsewhere = [lax.rem(mine + d, experts) for d in range(1, experts)]

    def remote(src, dst, send_sem, recv_sem, peer):
        return pltpu.make_async_remote_copy(
            src_ref=src, dst_ref=dst, send_sem=send_sem, recv_sem=recv_sem,
            device_id={"row": peer}, device_id_type=MESH,
        )

    def copy1(s, peer, land):
        return remote(out1.at[s, peer], in1.at[s, land], send1.at[s, peer], recv1.at[s, land], peer)

    def copy2(s, k, peer, land):
        return remote(
            out2.at[s, k, peer], in2.at[s, k, land], send2.at[s, k, peer], recv2.at[s, k, land], peer
        )

    def copy3(peer, land):
        return remote(peaks.at[me], peaks.at[land], send3.at[peer], recv3.at[land], peer)

    def copy4(peer, land):
        return remote(row_sums.at[me], row_sums.at[land], send4.at[peer], recv4.at[land], peer)

    def copy5(peer, land):
        return pltpu.make_async_remote_copy(
            src_ref=expert_sums.at[mine], dst_ref=expert_sums.at[land],
            send_sem=send5.at[peer], recv_sem=recv5.at[land],
            device_id={"expert": peer}, device_id_type=MESH,
        )

    barrier = pltpu.get_barrier_semaphore()
    for peer in others:
        pl.semaphore_signal(barrier, inc=1, device_id={"row": peer}, device_id_type=MESH)
    for peer in elsewhere:
        pl.semaphore_signal(barrier, inc=1, device_id={"expert": peer}, device_id_type=MESH)
    build_column(right_ref, h_ref, 1.0 / math.sqrt(width * HB))
    build_left(left_ref, left)
    load.wait()

    def column_side(peer, dst, place):
        def step(j, _):
            low = jnp.dot(x_ref[j, :, :half], h_ref[0, peer], preferred_element_type=jnp.float32)
            high = jnp.dot(x_ref[j, :, half:], h_ref[1, peer], preferred_element_type=jnp.float32)
            sign = jnp.concatenate([left[j]] * slabs, axis=1)
            for s, both in ((0, low + high), (1, low - high)):
                both = both * sign
                parts = fold_rows([both[k * SUB:(k + 1) * SUB] for k in range(FOLD)])
                for k in range(FOLD):
                    dst[s, place, k, pl.ds(pl.multiple_of(j * SUB, SUB), SUB), :] = parts[k].astype(jnp.bfloat16)
            return 0

        lax.fori_loop(0, blocks, step, 0)

    for step, peer in enumerate(others):
        column_side(peer, out1, peer)
        if step == 0:
            pl.semaphore_wait(barrier, peers + experts - 2)
        copy1(0, peer, me).start()
    for peer in others:
        copy1(1, peer, me).start()
    column_side(me, in1, me)
    build_row(cosine_ref, m_ref)
    build_order(p_ref)

    def row_side(s, send):
        for peer in others:
            copy1(s, peer, peer).wait_recv()

        def step(k, peak):
            z = in1[s, :, k].reshape(peers * rows, lanes)
            r = jnp.dot(m_ref[...], z, preferred_element_type=jnp.float32)
            out2[s, k] = r.astype(jnp.bfloat16).reshape(peers, rows, lanes)
            if send:
                for peer in others:
                    copy2(s, k, peer, me).start()
            return jnp.maximum(peak, jnp.max(jnp.abs(r).reshape(-1, 8, lanes), axis=0))

        peak = lax.fori_loop(0, FOLD, step, jnp.zeros((8, lanes), jnp.float32))
        peaks[me, s] = jnp.broadcast_to(jnp.max(peak, axis=0, keepdims=True), (8, lanes))

    row_side(0, True)
    row_side(1, False)
    for peer in others:
        copy3(peer, me).start()

    def send_second(k, _):
        for peer in others:
            copy2(1, k, peer, me).start()
        return 0

    lax.fori_loop(0, FOLD, send_second, 0)

    def keep_own(k, _):
        for s in range(2):
            in2[s, k, me] = out2[s, k, me]
        return 0

    lax.fori_loop(0, FOLD, keep_own, 0)

    for peer in others:
        copy3(peer, peer).wait_recv()
    column_peak = jnp.concatenate([peaks[q, s, 0:1, :] for s in range(2) for q in range(peers)], axis=1)
    spread = jnp.broadcast_to(group_ref[...], (8, width)).astype(jnp.float32).astype(jnp.bfloat16)
    group = jnp.concatenate([
        lax.dot_general(
            spread[:, s * half:(s + 1) * half], p_ref[...], (((1,), (1,)), ((), ())),
            preferred_element_type=jnp.float32,
        )[:1]
        for s in range(2)
    ], axis=1)
    column_scale = jnp.zeros_like(column_peak)
    group_scale = jnp.zeros((8, LANES), jnp.float32)
    lane = lax.broadcasted_iota(jnp.int32, (8, LANES), 1)
    for g in range(GROUPS):
        inside = group == float(g)
        peak = jnp.maximum(jnp.max(jnp.where(inside, column_peak, 0.0), axis=1, keepdims=True), 1.0)
        column_scale = jnp.where(inside, 2.0 / peak, column_scale)
        group_scale = jnp.where(lane == g, peak * 0.5, group_scale)
    scale_ref[...] = group_scale[:1, :GROUPS]
    sum_ref[...] = jnp.zeros_like(sum_ref)

    total_rows = peers * blocks * HB

    for s in range(2):
        scales = [
            column_scale[:, s * half + c * LANES:s * half + (c + 1) * LANES] for c in range(OCT)
        ]

        def lattice(k, _, s=s, scales=scales):
            for peer in others:
                copy2(s, k, peer, peer).wait_recv()

            def tile(j, _):
                at = pl.ds(pl.multiple_of(j * SUB, SUB), SUB)
                square = near = low = size = most = least = None
                for c in range(OCT):
                    q, part = c // slabs, c % slabs
                    rotated = in2[s, k, q, at, part * LANES:(part + 1) * LANES].astype(jnp.float32)
                    value = rotated * scales[c]
                    turned[at, c * LANES:(c + 1) * LANES] = value.astype(jnp.bfloat16)
                    nearest = jnp.round(value)
                    offset = jnp.abs(value - nearest)
                    below = jnp.floor(value)
                    if c == 0:
                        square, near, low, size = offset * offset, nearest, below, offset
                        most = least = offset
                    else:
                        square, near, low = square + offset * offset, near + nearest, low + below
                        size = size + offset
                        most, least = jnp.maximum(most, offset), jnp.minimum(least, offset)
                odd = near - 2.0 * jnp.floor(near * 0.5) > 0.5
                whole = jnp.where(odd, square + (1.0 - 2.0 * most), square)
                shifted = square + (OCT * 0.25 - size)
                odd = low - 2.0 * jnp.floor(low * 0.5) > 0.5
                error = jnp.minimum(whole, jnp.where(odd, shifted + 2.0 * least, shifted))
                error_ref[j, k, :, s * LANES:(s + 1) * LANES] = error
                row = me * (blocks * HB) + j * HB + k * SUB + lax.broadcasted_iota(jnp.int32, (SUB, LANES), 0)
                weight = (1.0 + 4.0 * (row.astype(jnp.float32) + 0.5) / total_rows) / 3.0
                sum_ref[...] += error * weight
                return 0

            lax.fori_loop(0, blocks, tile, 0)
            natural = jnp.dot(turned[...], p_ref[...], preferred_element_type=jnp.float32)
            scaled_ref[:, k, :, s * half:(s + 1) * half] = natural.astype(jnp.bfloat16).reshape(blocks, SUB, half)
            return 0

        lax.fori_loop(0, FOLD, lattice, 0)

    part = jnp.sum(jnp.sum(sum_ref[...], axis=0, keepdims=True), axis=1, keepdims=True)
    row_sums[me] = jnp.broadcast_to(part / (total_rows * width // OCT), (8, LANES))
    for peer in others:
        copy4(peer, me).start()
    for peer in others:
        copy4(peer, peer).wait_recv()
    mean = row_sums[0]
    for q in range(1, peers):
        mean = mean + row_sums[q]
    expert_sums[mine] = mean
    for peer in elsewhere:
        copy5(peer, mine).start()
    for peer in elsewhere:
        copy5(peer, peer).wait_recv()
    total = expert_sums[0]
    for e in range(1, experts):
        total = total + expert_sums[e]
    mean_ref[0] = jnp.max(mean)
    total_ref[0] = jnp.max(total / experts)

    for s in range(2):
        for peer in others:
            copy1(s, peer, me).wait_send()
    for peer in others:
        copy3(peer, me).wait_send()
        copy4(peer, me).wait_send()
    for peer in elsewhere:
        copy5(peer, mine).wait_send()

    def drain(k, _):
        for s in range(2):
            for peer in others:
                copy2(s, k, peer, me).wait_send()
        return 0

    lax.fori_loop(0, FOLD, drain, 0)


def put_kernel(scaled_ref, error_ref, scaled_out, error_out, sems):
    copies = (
        pltpu.make_async_copy(scaled_ref, scaled_out, sems.at[0]),
        pltpu.make_async_copy(error_ref, error_out, sems.at[1]),
    )
    for copy in copies:
        copy.start()
    for copy in copies:
        copy.wait()


def put(scaled, errors):
    return pl.pallas_call(
        put_kernel,
        out_shape=(
            jax.ShapeDtypeStruct(scaled.shape, scaled.dtype),
            jax.ShapeDtypeStruct(errors.shape, errors.dtype),
        ),
        in_specs=[pl.BlockSpec(memory_space=pltpu.VMEM)] * 2,
        out_specs=[pl.BlockSpec(memory_space=pl.ANY)] * 2,
        scratch_shapes=[pltpu.SemaphoreType.DMA((2,))],
        compiler_params=pltpu.CompilerParams(vmem_limit_bytes=16 * 2**20),
    )(scaled, errors)


def body(weights, left_bits, right_bits, groups):
    _, local_rows, width = weights.shape
    peers = lax.axis_size("row")
    experts = lax.axis_size("expert")
    blocks = local_rows // HB
    half = width // 2
    lanes = half // peers
    rows = blocks * SUB
    cosine = cosine_block(BLOCKS).astype(jnp.bfloat16)
    vmem = pl.BlockSpec(memory_space=pltpu.VMEM)
    hbm = pl.BlockSpec(memory_space=pl.ANY)
    dma = pltpu.SemaphoreType.DMA
    smem = pl.BlockSpec(memory_space=pltpu.SMEM)
    scaled, errors, group_scale, mean, total = pl.pallas_call(
        functools.partial(kernel, peers, experts),
        out_shape=(
            pltpu.VMEM((blocks, FOLD, SUB, width), jnp.bfloat16),
            pltpu.VMEM((blocks, FOLD, SUB, width // OCT), jnp.float32),
            jax.ShapeDtypeStruct((1, GROUPS), jnp.float32),
            jax.ShapeDtypeStruct((1,), jnp.float32),
            jax.ShapeDtypeStruct((1,), jnp.float32),
        ),
        in_specs=[hbm] + [vmem] * 4,
        out_specs=(vmem, vmem, vmem, smem, smem),
        scratch_shapes=[
            pltpu.VMEM((blocks, HB, width), jnp.bfloat16),
            pltpu.VMEM((blocks, HB, LANES), jnp.float32),
            pltpu.VMEM((2, peers, half, lanes), jnp.bfloat16),
            pltpu.VMEM((BLOCKS * SUB, BLOCKS * SUB), jnp.bfloat16),
            pltpu.VMEM((half, half), jnp.bfloat16),
            pltpu.VMEM((2, peers, FOLD, rows, lanes), jnp.bfloat16),
            pltpu.VMEM((2, peers, FOLD, rows, lanes), jnp.bfloat16),
            pltpu.VMEM((2, FOLD, peers, rows, lanes), jnp.bfloat16),
            pltpu.VMEM((2, FOLD, peers, rows, lanes), jnp.bfloat16),
            pltpu.VMEM((peers, 2, 8, lanes), jnp.float32),
            pltpu.VMEM((rows, half), jnp.bfloat16),
            pltpu.VMEM((SUB, LANES), jnp.float32),
            pltpu.VMEM((peers, 8, LANES), jnp.float32),
            pltpu.VMEM((experts, 8, LANES), jnp.float32),
            dma((2, peers)),
            dma((2, peers)),
            dma((2, FOLD, peers)),
            dma((2, FOLD, peers)),
            dma((peers,)),
            dma((peers,)),
            dma((peers,)),
            dma((peers,)),
            dma((experts,)),
            dma((experts,)),
            dma,
        ],
        compiler_params=pltpu.CompilerParams(
            collective_id=0, has_side_effects=True, vmem_limit_bytes=48 * 2**20
        ),
    )(weights.reshape(blocks, HB, width), left_bits, right_bits, groups, cosine)
    scaled, errors = put(scaled, errors)
    return (
        scaled.reshape(1, local_rows, width),
        errors.reshape(1, local_rows, width // OCT),
        group_scale,
        mean,
        total.reshape(()),
    )


def solution(mesh):
    placed = (P("expert", "row", None), P("expert", "row"), P("expert", None), P("expert", None))
    return jax.shard_map(
        body,
        mesh=mesh,
        in_specs=placed,
        out_specs=(
            P("expert", "row", None),
            P("expert", "row", None),
            P("expert", None),
            P("expert"),
            P(),
        ),
        check_vma=False,
    )
```

profile of v0, /device:TPU:0, one launch (start us, length us, event | category | flops | bytes accessed | tf_op | source)
XLA Modules:
  0.0 348.9 jit_solution(5953702560175287773)
XLA Ops:
  0.7 0.7 select_convert_fusion.cosine_ref
  1.4 339.8 %shard_map.83 = (bf16[14,8,16,2048]{3,2,1,0:T(8,128)(2,1)S(1)}, f32[14,8,16,256]{3,2,1,0:T(8,128)S(1)}, f32[1,16]{1,0:T(1,128)}, f32[1]{0:T(128)}, f32[1]{0:T(128)}) custom-call(bf16[14,128,2048]{2,1,0:T(8,128)(2,1)} %bitcast.4, s32[1,1792]{1,0:T(1,128)} %left_ref.1, s32[1,2048]{1,0:T(1,128)} %right_ref.1, s32[1,2048]{1,0:T(1,128)} %group_ref.1, ...), custom_call_target="tpu_custom_call" | custom-call | tf_op jit(solution)/shard_map/pallas_call | solution.py:376
  341.2 0.0 copy-start
  341.2 3.7 %shard_map.84 = (bf16[14,8,16,2048]{3,2,1,0:T(8,128)(2,1)}, f32[14,8,16,256]{3,2,1,0:T(8,128)}) custom-call(bf16[14,8,16,2048]{3,2,1,0:T(8,128)(2,1)S(1)} %get-tuple-element.12.scaled_ref, f32[14,8,16,256]{3,2,1,0:T(8,128)S(1)} %get-tuple-element.13.error_ref), custom_call_target="tpu_custom_call" | custom-call | tf_op jit(solution)/shard_map/pallas_call | solution.py:350
  344.9 0.0 copy-done
  344.9 0.5 copy.12
  (2 shorter events, 0.0 us)
Async XLA Ops:
  341.2 3.7 %copy-start = (f32[1,16]{1,0:T(1,128)S(1)}, f32[1,16]{1,0:T(1,128)}, u32[]{:S(2)}) copy-start(f32[1,16]{1,0:T(1,128)} %get-tuple-element.26) | copy-start | bytes 196
where the time goes:
time: 349 us
  Pallas kernels  343 us (98%)
  between operations  4.15 us (1%)
    pallas_call x1, Pallas kernels, body(): pl.pallas_call(functools.partial(kernel, peers, experts), out_shape=(pltp...  340 us

commit v1 on v0

v1 whole, which is shorter than its diff:
```python
import functools
import math

import jax
import jax.numpy as jnp
import numpy as np
from jax import lax
from jax.experimental import pallas as pl
from jax.experimental.pallas import tpu as pltpu
from jax.sharding import PartitionSpec as P

HB = 128
SUB = 16
FOLD = HB // SUB
OCT = 8
LANES = 128
GROUPS = 16
BLOCKS = 56
SLAB = 256
PACK = LANES * OCT // SLAB
MESH = pl.DeviceIdType.MESH


def signs(common, bits):
    for shift in (4, 2, 1):
        if shift < bits:
            common = common ^ (common >> shift)
    return (1 - 2 * (common & 1)).astype(jnp.float32)


def iota(shape, dim):
    return lax.broadcasted_iota(jnp.int32, shape, dim)


def down(row):
    return jnp.broadcast_to(row, (LANES, LANES)).T


def cosine_table(order):
    first = np.arange(order, dtype=np.float64)[:, None]
    second = np.arange(order, dtype=np.float64)[None, :]
    table = math.sqrt(2.0 / order) * np.cos(math.pi * (2.0 * second + 1.0) * first / (2.0 * order))
    return np.where(first == 0.0, table * math.sqrt(0.5), table)


def cross_factors(order, to):
    half = order // 2
    block = cosine_table(order)[to * half:(to + 1) * half, (1 - to) * half:(2 - to) * half]
    even, odd = block[0::2], block[1::2]
    along = odd @ even.T / np.sum(even * even, axis=1)
    u, s, v = np.linalg.svd(odd - along @ even)
    kept = int(np.sum(s > 2.0 ** -24))
    v, u = v[:kept], u[:, :kept] * s[:kept]
    flip = np.sign(np.take_along_axis(v, np.argmax(np.abs(v), axis=1)[:, None], axis=1))
    count = even.shape[0]
    gather = np.concatenate([even, v * flip])
    spread = np.zeros((half, count + kept))
    spread[0::2, :count] = np.eye(count)
    spread[1::2, :count] = along
    spread[1::2, count:] = u * flip[:, 0]
    return gather, spread


def row_tables(order):
    half = order // 2
    table = cosine_table(order)
    near = np.stack([table[s * half:(s + 1) * half, s * half:(s + 1) * half] for s in range(2)])
    to_low, to_high = cross_factors(order, 0), cross_factors(order, 1)
    gather = np.stack([to_high[0], to_low[0]])
    spread = np.stack([to_low[1], to_high[1]])
    return tuple(jnp.asarray(t, jnp.float32).astype(jnp.bfloat16) for t in (near, gather, spread))


def build_column(right_ref, h_ref, scale):
    half = h_ref.shape[2]
    square = (LANES, LANES)
    inner = signs(iota(square, 0) & iota(square, 1), 7)

    def step(u, _):
        at = pl.ds(pl.multiple_of(u * LANES, LANES), LANES)
        for side in range(2):
            bits = right_ref[:, pl.ds(pl.multiple_of(side * half + u * LANES, LANES), LANES)]
            part = inner * down((2 * bits - 1).astype(jnp.float32) * scale)
            for v in range(half // LANES):
                common = u & v
                common = common ^ (common >> 4)
                common = common ^ (common >> 2)
                common = common ^ (common >> 1)
                sign = (1 - 2 * (common & 1)).astype(jnp.float32)
                q, c = v * LANES // SLAB, v * LANES % SLAB
                h_ref[side, q, at, c:c + LANES] = (part * sign).astype(jnp.bfloat16)
        return 0

    lax.fori_loop(0, half // LANES, step, 0)


def build_left(left_ref, left):
    def step(j, _):
        bits = left_ref[:, pl.ds(pl.multiple_of(j * HB, HB), HB)]
        left[j] = down((2 * bits - 1).astype(jnp.float32))
        return 0

    lax.fori_loop(0, left.shape[0], step, 0)


def expand(table, out_ref, mixed):
    high, wide = table.shape
    cuts = next(d for d in range(1, high + 1) if high % d == 0 and high // d * SUB <= LANES)
    chunk = high // cuts * SUB
    size = wide * SUB
    spread = (iota((size, wide), 0) // SUB == iota((size, wide), 1)).astype(jnp.float32).astype(jnp.bfloat16)
    if mixed:
        small = signs((iota((chunk, size), 0) & iota((chunk, size), 1)) & (SUB - 1), 4)
    else:
        small = (((iota((chunk, size), 0) ^ iota((chunk, size), 1)) & (SUB - 1)) == 0).astype(jnp.float32)

    def step(u, _):
        at = pl.multiple_of(u * chunk, chunk)
        here = ((at + iota((chunk, high), 0)) // SUB == iota((chunk, high), 1)).astype(jnp.float32)
        rows = jnp.dot(here.astype(jnp.bfloat16), table, preferred_element_type=jnp.float32)
        full = lax.dot_general(
            rows.astype(jnp.bfloat16), spread, (((1,), (1,)), ((), ())), preferred_element_type=jnp.float32
        )
        out_ref[pl.ds(at, chunk), :] = (full * small).astype(jnp.bfloat16)
        return 0

    lax.fori_loop(0, cuts, step, 0)


def build_order(p_ref):
    size = p_ref.shape[0]
    octets = SLAB // OCT

    def step(s, _):
        lane = iota((size, LANES), 1)
        wanted = lane // octets * SLAB + lane % octets * OCT + s
        hit = (wanted == iota((size, LANES), 0)).astype(jnp.float32)
        p_ref[:, pl.ds(pl.multiple_of(s * LANES, LANES), LANES)] = hit.astype(jnp.bfloat16)
        return 0

    lax.fori_loop(0, OCT, step, 0)


def fold_rows(parts):
    step = 1
    while step < len(parts):
        mixed = list(parts)
        for k in range(len(parts)):
            if not k & step:
                mixed[k] = parts[k] + parts[k + step]
                mixed[k + step] = parts[k] - parts[k + step]
        parts, step = mixed, 2 * step
    return parts


def loop(count, step):
    def run(i, _):
        step(i)
        return 0

    lax.fori_loop(0, count, run, 0)


def kernel(
    peers, experts, x_hbm, left_ref, right_ref, group_ref, near_ref, gather_ref, spread_ref,
    scaled_ref, error_ref, scale_ref, mean_ref, total_ref,
    x_ref, left, h_ref, near, gather, spread, p_ref, cols, out_s, in_s, planar_ref, planar_group, peaks,
    sum_ref, row_sums, expert_sums,
    send1, recv1, send2, recv2, send3, recv3, send_s, recv_s, send4, recv4, send5, recv5, load_sem,
):
    blocks, _, width = x_ref.shape
    half = width // 2
    slabs = width // SLAB
    pairs = slabs // 2
    mates = peers // 2
    rows = blocks * SUB
    me = lax.axis_index("row")
    mine = lax.axis_index("expert")
    side = me // mates
    slot = me - side * mates
    hub = mates - 1 + side
    far_hub = mates - side
    is_hub = me == hub
    hub_slot = hub - side * mates
    load = pltpu.make_async_copy(x_hbm, x_ref, load_sem)
    load.start()
    others = [lax.rem(me + d, peers) for d in range(1, peers)]
    elsewhere = [lax.rem(mine + d, experts) for d in range(1, experts)]
    mate_slots = [lax.rem(hub_slot + d, mates) for d in range(1, mates)]

    def remote(src, dst, send_sem, recv_sem, peer):
        return pltpu.make_async_remote_copy(
            src_ref=src, dst_ref=dst, send_sem=send_sem, recv_sem=recv_sem,
            device_id={"row": peer}, device_id_type=MESH,
        )

    def to_hub(s, k, who):
        piece = cols.at[s, k, who]
        return remote(piece, piece, send1.at[s, k], recv1.at[s, k, who], hub)

    def from_hub(s, k, who):
        return remote(
            cols.at[s, k, who], cols.at[s, k, hub_slot], send2.at[s, k, who], recv2.at[s, k],
            side * mates + who,
        )

    def across(s, k):
        return remote(out_s.at[s, k], in_s.at[s, k], send_s.at[s, k], recv_s.at[s, k], far_hub)

    def share_peak(t, s, peer):
        piece = peaks.at[t, s]
        return remote(piece, piece, send3.at[s, peer], recv3.at[t, s], peer)

    def copy4(peer, land):
        return remote(row_sums.at[me], row_sums.at[land], send4.at[peer], recv4.at[land], peer)

    def copy5(peer, land):
        return pltpu.make_async_remote_copy(
            src_ref=expert_sums.at[mine], dst_ref=expert_sums.at[land],
            send_sem=send5.at[peer], recv_sem=recv5.at[land],
            device_id={"expert": peer}, device_id_type=MESH,
        )

    barrier = pltpu.get_barrier_semaphore()
    for peer in others:
        pl.semaphore_signal(barrier, inc=1, device_id={"row": peer}, device_id_type=MESH)
    for peer in elsewhere:
        pl.semaphore_signal(barrier, inc=1, device_id={"expert": peer}, device_id_type=MESH)
    build_column(right_ref, h_ref, 1.0 / math.sqrt(width * HB))
    build_left(left_ref, left)
    load.wait()

    def column_side(q):
        def step(j):
            low = jnp.dot(x_ref[j, :, :half], h_ref[0, q], preferred_element_type=jnp.float32)
            high = jnp.dot(x_ref[j, :, half:], h_ref[1, q], preferred_element_type=jnp.float32)
            sign = jnp.concatenate([left[j]] * (SLAB // LANES), axis=1)
            for s, both in ((q, low + high), (q + pairs, low - high)):
                both = both * sign
                parts = fold_rows([both[k * SUB:(k + 1) * SUB] for k in range(FOLD)])
                for k in range(FOLD):
                    cols[s, k, slot, pl.ds(pl.multiple_of(j * SUB, SUB), SUB), :] = parts[k].astype(jnp.bfloat16)

        loop(blocks, step)

    def send_slab(s):
        loop(FOLD, lambda k: to_hub(s, k, slot).start())

    def forward(s, k):
        for who in mate_slots:
            to_hub(s, k, who).wait_recv()
        z = cols[s, k].reshape(mates * rows, SLAB)
        r = jnp.dot(gather[...], z, preferred_element_type=jnp.float32)
        out_s[s, k] = r.astype(jnp.bfloat16)
        across(s, k).start()

    def backward(s, k, peak):
        across(s, k).wait_recv()
        z = cols[s, k].reshape(mates * rows, SLAB)
        r = jnp.dot(near[...], z, preferred_element_type=jnp.float32)
        r = r + jnp.dot(spread[...], in_s[s, k], preferred_element_type=jnp.float32)
        cols[s, k] = r.astype(jnp.bfloat16).reshape(mates, rows, SLAB)
        for who in mate_slots:
            from_hub(s, k, who).start()
        return jnp.maximum(peak, jnp.max(jnp.abs(r).reshape(-1, 8, SLAB), axis=0))

    def group_scale(first, count):
        span = count * SLAB
        slab = [jnp.clip(first + i, 0, slabs - 1) for i in range(count)]
        top = jnp.concatenate([jnp.maximum(peaks[0, t], peaks[1, t])[:1] for t in slab], axis=1)
        group = jnp.concatenate(
            [group_ref[:, pl.ds(pl.multiple_of(t * SLAB, SLAB), SLAB)] for t in slab], axis=1
        )
        inside = group == iota((GROUPS, span), 0)
        return jnp.maximum(jnp.max(jnp.where(inside, top, 0.0), axis=1, keepdims=True), 1.0)

    total_rows = peers * blocks * HB

    def lattice(s):
        last = jnp.minimum(s + 1, slabs - 1)

        def peak_in(t):
            @pl.when(jnp.logical_or(jnp.logical_not(is_hub), side != t))
            def _():
                def wait(n):
                    share_peak(t, n, me).wait_recv()

                @pl.when(s == 0)
                def _():
                    wait(0)

                @pl.when(s + 1 < slabs)
                def _():
                    wait(last)

        for t in range(2):
            peak_in(t)
        factor = 2.0 / group_scale(s - 1, 3)
        at_slab = pl.ds(pl.multiple_of(s * SLAB, SLAB), SLAB)
        wide = group_ref[:, at_slab] == iota((GROUPS, SLAB), 0)
        natural = jnp.max(jnp.where(wide, factor, 0.0), axis=0, keepdims=True)
        wide = planar_group[s] == iota((GROUPS, OCT * LANES), 0).astype(jnp.float32)
        planar = jnp.max(jnp.where(wide, factor, 0.0), axis=0, keepdims=True)
        scales = [planar[:, c * LANES:(c + 1) * LANES] for c in range(OCT)]
        octets = SLAB // OCT
        lane = iota((SUB, LANES), 1)
        place = s % PACK
        here = lane // octets == place
        at_error = pl.ds(pl.multiple_of(s // PACK * LANES, LANES), LANES)

        def part(kk):
            @pl.when(jnp.logical_not(is_hub))
            def _():
                for g in range(PACK):
                    from_hub(s, kk * PACK + g, slot).wait_recv()

            both = jnp.concatenate([cols[s, kk * PACK + g, hub_slot] for g in range(PACK)], axis=1)
            planar_ref[...] = jnp.dot(both, p_ref[...], preferred_element_type=jnp.float32)

            def tile(j):
                at = pl.ds(pl.multiple_of(j * SUB, SUB), SUB)
                for g in range(PACK):
                    value = cols[s, kk * PACK + g, hub_slot, at, :].astype(jnp.float32) * natural
                    scaled_ref[j, kk * PACK + g, :, at_slab] = value.astype(jnp.bfloat16)
                square = near_sum = low = size = most = least = None
                for c in range(OCT):
                    value = planar_ref[at, c * LANES:(c + 1) * LANES] * scales[c]
                    nearest = jnp.round(value)
                    offset = jnp.abs(value - nearest)
                    below = jnp.floor(value)
                    if c == 0:
                        square, near_sum, low, size = offset * offset, nearest, below, offset
                        most = least = offset
                    else:
                        square, near_sum, low = square + offset * offset, near_sum + nearest, low + below
                        size = size + offset
                        most, least = jnp.maximum(most, offset), jnp.minimum(least, offset)
                odd = near_sum - 2.0 * jnp.floor(near_sum * 0.5) > 0.5
                whole = jnp.where(odd, square + (1.0 - 2.0 * most), square)
                shifted = square + (OCT * 0.25 - size)
                odd = low - 2.0 * jnp.floor(low * 0.5) > 0.5
                error = jnp.minimum(whole, jnp.where(odd, shifted + 2.0 * least, shifted))
                row = me * (blocks * HB) + j * HB + (kk * PACK + lane // octets) * SUB + iota((SUB, LANES), 0)
                weight = (1.0 + 4.0 * (row.astype(jnp.float32) + 0.5) / total_rows) / 3.0
                sum_ref[...] += error * weight
                for g in range(PACK):
                    turned = pltpu.roll(error, lax.rem(place + PACK - g, PACK) * octets, 1)
                    old = error_ref[j, kk * PACK + g, :, at_error]
                    error_ref[j, kk * PACK + g, :, at_error] = jnp.where(here, turned, old)

            loop(blocks, tile)

        loop(FOLD // PACK, part)

    column_side(0)
    pl.semaphore_wait(barrier, peers + experts - 2)

    @pl.when(jnp.logical_not(is_hub))
    def _():
        send_slab(0)

        def step(q):
            column_side(q + 1)
            send_slab(q + 1)

        loop(pairs - 1, step)
        loop(slabs - pairs, lambda q: send_slab(q + pairs))

    @pl.when(is_hub)
    def _():
        expand(gather_ref[side], gather, True)
        expand(near_ref[side], near, True)
        expand(spread_ref[side], spread, False)
        loop(FOLD, lambda k: forward(0, k))

    build_order(p_ref)
    sum_ref[...] = jnp.zeros_like(sum_ref)

    def group_order(s):
        row = group_ref[:, pl.ds(pl.multiple_of(s * SLAB, SLAB), SLAB)].astype(jnp.float32)
        row = jnp.concatenate([jnp.broadcast_to(row, (SUB, SLAB)).astype(jnp.bfloat16)] * PACK, axis=1)
        planar_group[s] = jnp.dot(row, p_ref[...], preferred_element_type=jnp.float32)[:1]

    loop(slabs, group_order)

    def stage(t):
        @pl.when(jnp.logical_and(is_hub, t + 1 < pairs))
        def _():
            column_side(t + 1)

        @pl.when(t >= 2)
        def _():
            lattice(t - 2)

        @pl.when(jnp.logical_and(is_hub, t < slabs))
        def _():
            def step(k, peak):
                @pl.when(t + 1 < slabs)
                def _():
                    forward(t + 1, k)

                return backward(t, k, peak)

            peak = lax.fori_loop(0, FOLD, step, jnp.zeros((8, SLAB), jnp.float32))
            peaks[side, t] = jnp.broadcast_to(jnp.max(peak, axis=0, keepdims=True), (8, SLAB))
            for peer in others:
                share_peak(side, t, peer).start()

    loop(slabs + 2, stage)

    peak = group_scale(0, slabs) * 0.5
    scale_ref[...] = jnp.broadcast_to(peak, (GROUPS, LANES)).T[:1, :GROUPS]

    part = jnp.sum(jnp.sum(sum_ref[...], axis=0, keepdims=True), axis=1, keepdims=True)
    row_sums[me] = jnp.broadcast_to(part / (total_rows * width // OCT), (8, LANES))
    for peer in others:
        copy4(peer, me).start()
    for peer in others:
        copy4(peer, peer).wait_recv()
    mean = row_sums[0]
    for q in range(1, peers):
        mean = mean + row_sums[q]
    expert_sums[mine] = mean
    for peer in elsewhere:
        copy5(peer, mine).start()
    for peer in elsewhere:
        copy5(peer, peer).wait_recv()
    total = expert_sums[0]
    for e in range(1, experts):
        total = total + expert_sums[e]
    mean_ref[0] = jnp.max(mean)
    total_ref[0] = jnp.max(total / experts)

    @pl.when(jnp.logical_not(is_hub))
    def _():
        loop(slabs, lambda s: loop(FOLD, lambda k: to_hub(s, k, slot).wait_send()))

    @pl.when(is_hub)
    def _():
        def drain(s):
            for peer in others:
                share_peak(side, s, peer).wait_send()

            def step(k):
                across(s, k).wait_send()
                for who in mate_slots:
                    from_hub(s, k, who).wait_send()

            loop(FOLD, step)

        loop(slabs, drain)

    for peer in others:
        copy4(peer, me).wait_send()
    for peer in elsewhere:
        copy5(peer, mine).wait_send()


def put_kernel(scaled_ref, error_ref, scaled_out, error_out, sems):
    copies = (
        pltpu.make_async_copy(scaled_ref, scaled_out, sems.at[0]),
        pltpu.make_async_copy(error_ref, error_out, sems.at[1]),
    )
    for copy in copies:
        copy.start()
    for copy in copies:
        copy.wait()


def put(scaled, errors):
    return pl.pallas_call(
        put_kernel,
        out_shape=(
            jax.ShapeDtypeStruct(scaled.shape, scaled.dtype),
            jax.ShapeDtypeStruct(errors.shape, errors.dtype),
        ),
        in_specs=[pl.BlockSpec(memory_space=pltpu.VMEM)] * 2,
        out_specs=[pl.BlockSpec(memory_space=pl.ANY)] * 2,
        scratch_shapes=[pltpu.SemaphoreType.DMA((2,))],
        compiler_params=pltpu.CompilerParams(vmem_limit_bytes=16 * 2**20),
    )(scaled, errors)


def body(weights, left_bits, right_bits, groups):
    _, local_rows, width = weights.shape
    peers = lax.axis_size("row")
    experts = lax.axis_size("expert")
    blocks = local_rows // HB
    half = width // 2
    mates = peers // 2
    rows = blocks * SUB
    slabs = width // SLAB
    near, gather, spread = row_tables(BLOCKS)
    inner, reach = mates * rows, gather.shape[1] * SUB
    vmem = pl.BlockSpec(memory_space=pltpu.VMEM)
    hbm = pl.BlockSpec(memory_space=pl.ANY)
    dma = pltpu.SemaphoreType.DMA
    smem = pl.BlockSpec(memory_space=pltpu.SMEM)
    scaled, errors, group_scale, mean, total = pl.pallas_call(
        functools.partial(kernel, peers, experts),
        out_shape=(
            pltpu.VMEM((blocks, FOLD, SUB, width), jnp.bfloat16),
            pltpu.VMEM((blocks, FOLD, SUB, width // OCT), jnp.float32),
            jax.ShapeDtypeStruct((1, GROUPS), jnp.float32),
            jax.ShapeDtypeStruct((1,), jnp.float32),
            jax.ShapeDtypeStruct((1,), jnp.float32),
        ),
        in_specs=[hbm] + [vmem] * 6,
        out_specs=(vmem, vmem, vmem, smem, smem),
        scratch_shapes=[
            pltpu.VMEM((blocks, HB, width), jnp.bfloat16),
            pltpu.VMEM((blocks, HB, LANES), jnp.float32),
            pltpu.VMEM((2, slabs // 2, half, SLAB), jnp.bfloat16),
            pltpu.VMEM((inner, inner), jnp.bfloat16),
            pltpu.VMEM((reach, inner), jnp.bfloat16),
            pltpu.VMEM((inner, reach), jnp.bfloat16),
            pltpu.VMEM((PACK * SLAB, OCT * LANES), jnp.bfloat16),
            pltpu.VMEM((slabs, FOLD, mates, rows, SLAB), jnp.bfloat16),
            pltpu.VMEM((slabs, FOLD, reach, SLAB), jnp.bfloat16),
            pltpu.VMEM((slabs, FOLD, reach, SLAB), jnp.bfloat16),
            pltpu.VMEM((rows, OCT * LANES), jnp.float32),
            pltpu.VMEM((slabs, 1, OCT * LANES), jnp.float32),
            pltpu.VMEM((2, slabs, 8, SLAB), jnp.float32),
            pltpu.VMEM((SUB, LANES), jnp.float32),
            pltpu.VMEM((peers, 8, LANES), jnp.float32),
            pltpu.VMEM((experts, 8, LANES), jnp.float32),
            dma((slabs, FOLD)),
            dma((slabs, FOLD, mates)),
            dma((slabs, FOLD, mates)),
            dma((slabs, FOLD)),
            dma((slabs, peers)),
            dma((2, slabs)),
            dma((slabs, FOLD)),
            dma((slabs, FOLD)),
            dma((peers,)),
            dma((peers,)),
            dma((experts,)),
            dma((experts,)),
            dma,
        ],
        compiler_params=pltpu.CompilerParams(
            collective_id=0, has_side_effects=True, vmem_limit_bytes=54 * 2**20
        ),
    )(weights.reshape(blocks, HB, width), left_bits, right_bits, groups, near, gather, spread)
    scaled, errors = put(scaled, errors)
    return (
        scaled.reshape(1, local_rows, width),
        errors.reshape(1, local_rows, width // OCT),
        group_scale,
        mean,
        total.reshape(()),
    )


def solution(mesh):
    placed = (P("expert", "row", None), P("expert", "row"), P("expert", None), P("expert", None))
    return jax.shard_map(
        body,
        mesh=mesh,
        in_specs=placed,
        out_specs=(
            P("expert", "row", None),
            P("expert", "row", None),
            P("expert", None),
            P("expert"),
            P(),
        ),
        check_vma=False,
    )
```

time: 349 us -> 319 us (0.914)
  Pallas kernels: 343 us -> 314 us
    pallas_call x1, Pallas kernels: 340 us -> 311 us  [body(): pl.pallas_call(functools.partial(kernel, peers, experts), out_shape=(pltp...]
where the time goes in v1:
time: 319 us
  Pallas kernels  314 us (98%)
  between operations  4.15 us (1%)
    pallas_call x1, Pallas kernels, body(): pl.pallas_call(functools.partial(kernel, peers, experts), out_shape=(pltp...  311 us

profile of v1, /device:TPU:0, one launch (start us, length us, event | category | flops | bytes accessed | tf_op | source)
XLA Modules:
  0.0 319.0 jit_solution(4256597251008933255)
XLA Ops:
  0.6 310.7 %shard_map.110 = (bf16[14,8,16,2048]{3,2,1,0:T(8,128)(2,1)S(1)}, f32[14,8,16,256]{3,2,1,0:T(8,128)S(1)}, f32[1,16]{1,0:T(1,128)}, f32[1]{0:T(128)}, f32[1]{0:T(128)}) custom-call(bf16[14,128,2048]{2,1,0:T(8,128)(2,1)} %bitcast.4, s32[1,1792]{1,0:T(1,128)} %left_ref.1, s32[1,2048]{1,0:T(1,128)} %right_ref.1, s32[1,2048]{1,0:T(1,128)} %group_ref.1, ...), custom_call_target="tpu_custom_call" | custom-call | tf_op jit(solution)/shard_map/pallas_call | solution.py:499
  311.3 0.0 copy-start
  311.3 3.7 %shard_map.111 = (bf16[14,8,16,2048]{3,2,1,0:T(8,128)(2,1)}, f32[14,8,16,256]{3,2,1,0:T(8,128)}) custom-call(bf16[14,8,16,2048]{3,2,1,0:T(8,128)(2,1)S(1)} %get-tuple-element.12.scaled_ref, f32[14,8,16,256]{3,2,1,0:T(8,128)S(1)} %get-tuple-element.13.error_ref), custom_call_target="tpu_custom_call" | custom-call | tf_op jit(solution)/shard_map/pallas_call | solution.py:471
  315.0 0.0 copy-done
  315.0 0.5 copy.15
Async XLA Ops:
  311.3 3.7 %copy-start = (f32[1,16]{1,0:T(1,128)S(1)}, f32[1,16]{1,0:T(1,128)}, u32[]{:S(2)}) copy-start(f32[1,16]{1,0:T(1,128)} %get-tuple-element.26) | copy-start | bytes 196

commit v2 on v1

--- a/solution.py
+++ b/solution.py
@@ -18,6 +18,7 @@
 BLOCKS = 56
 SLAB = 256
 PACK = LANES * OCT // SLAB
+LEAD = 3
 MESH = pl.DeviceIdType.MESH
 
 
@@ -68,7 +69,12 @@
     to_low, to_high = cross_factors(order, 0), cross_factors(order, 1)
     gather = np.stack([to_high[0], to_low[0]])
     spread = np.stack([to_low[1], to_high[1]])
-    return tuple(jnp.asarray(t, jnp.float32).astype(jnp.bfloat16) for t in (near, gather, spread))
+    index = np.arange(SUB)
+    inner = np.array([[1 - 2 * (bin(a & b).count("1") & 1) for b in index] for a in index], np.float32)
+    return tuple(
+        np.stack([np.kron(t, m) for t in ts]).astype(np.float32).astype(np.dtype(jnp.bfloat16))
+        for ts, m in ((near, inner), (gather, inner), (spread, np.eye(SUB, dtype=np.float32)))
+    )
 
 
 def build_column(right_ref, h_ref, scale):
@@ -103,30 +109,6 @@
     lax.fori_loop(0, left.shape[0], step, 0)
 
 
-def expand(table, out_ref, mixed):
-    high, wide = table.shape
-    cuts = next(d for d in range(1, high + 1) if high % d == 0 and high // d * SUB <= LANES)
-    chunk = high // cuts * SUB
-    size = wide * SUB
-    spread = (iota((size, wide), 0) // SUB == iota((size, wide), 1)).astype(jnp.float32).astype(jnp.bfloat16)
-    if mixed:
-        small = signs((iota((chunk, size), 0) & iota((chunk, size), 1)) & (SUB - 1), 4)
-    else:
-        small = (((iota((chunk, size), 0) ^ iota((chunk, size), 1)) & (SUB - 1)) == 0).astype(jnp.float32)
-
-    def step(u, _):
-        at = pl.multiple_of(u * chunk, chunk)
-        here = ((at + iota((chunk, high), 0)) // SUB == iota((chunk, high), 1)).astype(jnp.float32)
-        rows = jnp.dot(here.astype(jnp.bfloat16), table, preferred_element_type=jnp.float32)
-        full = lax.dot_general(
-            rows.astype(jnp.bfloat16), spread, (((1,), (1,)), ((), ())), preferred_element_type=jnp.float32
-        )
-        out_ref[pl.ds(at, chunk), :] = (full * small).astype(jnp.bfloat16)
-        return 0
-
-    lax.fori_loop(0, cuts, step, 0)
-
-
 def build_order(p_ref):
     size = p_ref.shape[0]
     octets = SLAB // OCT
@@ -162,11 +144,12 @@
 
 
 def kernel(
-    peers, experts, x_hbm, left_ref, right_ref, group_ref, near_ref, gather_ref, spread_ref,
+    peers, experts, x_hbm, left_hbm, right_hbm, group_hbm, near_hbm, gather_hbm, spread_hbm,
     scaled_ref, error_ref, scale_ref, mean_ref, total_ref,
-    x_ref, left, h_ref, near, gather, spread, p_ref, cols, out_s, in_s, planar_ref, planar_group, peaks,
-    sum_ref, row_sums, expert_sums,
-    send1, recv1, send2, recv2, send3, recv3, send_s, recv_s, send4, recv4, send5, recv5, load_sem,
+    x_ref, left_ref, right_ref, group_ref, near, gather, spread,
+    left, h_ref, p_ref, cols, out_s, in_s, planar_ref, planar_group, peaks, peak_ref, natural_ref, factor_ref,
+    sum_ref, sums,
+    send1, recv1, send2, recv2, send3, recv3, send_s, recv_s, send4, recv4, load_sem,
 ):
     blocks, _, width = x_ref.shape
     half = width // 2
@@ -182,10 +165,18 @@
     far_hub = mates - side
     is_hub = me == hub
     hub_slot = hub - side * mates
-    load = pltpu.make_async_copy(x_hbm, x_ref, load_sem)
-    load.start()
+    loads = [
+        pltpu.make_async_copy(src, dst, load_sem.at[n])
+        for n, (src, dst) in enumerate((
+            (right_hbm, right_ref), (left_hbm, left_ref), (x_hbm, x_ref), (group_hbm, group_ref),
+            (gather_hbm.at[side], gather), (near_hbm.at[side], near), (spread_hbm.at[side], spread),
+        ))
+    ]
+    for load in loads:
+        load.start()
     others = [lax.rem(me + d, peers) for d in range(1, peers)]
-    elsewhere = [lax.rem(mine + d, experts) for d in range(1, experts)]
+    devices = peers * experts
+    here = mine * peers + me
     mate_slots = [lax.rem(hub_slot + d, mates) for d in range(1, mates)]
 
     def remote(src, dst, send_sem, recv_sem, peer):
@@ -211,24 +202,27 @@
         piece = peaks.at[t, s]
         return remote(piece, piece, send3.at[s, peer], recv3.at[t, s], peer)
 
-    def copy4(peer, land):
-        return remote(row_sums.at[me], row_sums.at[land], send4.at[peer], recv4.at[land], peer)
-
-    def copy5(peer, land):
+    def share_sum(n, land):
+        there = lax.rem(here + n, devices)
         return pltpu.make_async_remote_copy(
-            src_ref=expert_sums.at[mine], dst_ref=expert_sums.at[land],
-            send_sem=send5.at[peer], recv_sem=recv5.at[land],
-            device_id={"expert": peer}, device_id_type=MESH,
+            src_ref=sums.at[here], dst_ref=sums.at[land], send_sem=send4.at[there], recv_sem=recv4.at[land],
+            device_id={"expert": there // peers, "row": lax.rem(there, peers)}, device_id_type=MESH,
         )
 
     barrier = pltpu.get_barrier_semaphore()
-    for peer in others:
-        pl.semaphore_signal(barrier, inc=1, device_id={"row": peer}, device_id_type=MESH)
-    for peer in elsewhere:
-        pl.semaphore_signal(barrier, inc=1, device_id={"expert": peer}, device_id_type=MESH)
+
+    def greet(n):
+        there = lax.rem(here + n + 1, devices)
+        pl.semaphore_signal(
+            barrier, inc=1, device_id={"expert": there // peers, "row": lax.rem(there, peers)}, device_id_type=MESH
+        )
+
+    loop(devices - 1, greet)
+    loads[0].wait()
     build_column(right_ref, h_ref, 1.0 / math.sqrt(width * HB))
+    loads[1].wait()
     build_left(left_ref, left)
-    load.wait()
+    loads[2].wait()
 
     def column_side(q):
         def step(j):
@@ -254,7 +248,7 @@
         out_s[s, k] = r.astype(jnp.bfloat16)
         across(s, k).start()
 
-    def backward(s, k, peak):
+    def backward(s, k):
         across(s, k).wait_recv()
         z = cols[s, k].reshape(mates * rows, SLAB)
         r = jnp.dot(near[...], z, preferred_element_type=jnp.float32)
@@ -262,7 +256,7 @@
         cols[s, k] = r.astype(jnp.bfloat16).reshape(mates, rows, SLAB)
         for who in mate_slots:
             from_hub(s, k, who).start()
-        return jnp.maximum(peak, jnp.max(jnp.abs(r).reshape(-1, 8, SLAB), axis=0))
+        peak_ref[...] = jnp.maximum(peak_ref[...], jnp.max(jnp.abs(r).reshape(-1, 8, SLAB), axis=0))
 
     def group_scale(first, count):
         span = count * SLAB
@@ -275,85 +269,86 @@
         return jnp.maximum(jnp.max(jnp.where(inside, top, 0.0), axis=1, keepdims=True), 1.0)
 
     total_rows = peers * blocks * HB
-
-    def lattice(s):
+    unroll = next(u for u in (2, 1) if blocks % u == 0)
+
+    def scale_slab(s):
         last = jnp.minimum(s + 1, slabs - 1)
 
         def peak_in(t):
             @pl.when(jnp.logical_or(jnp.logical_not(is_hub), side != t))
             def _():
-                def wait(n):
-                    share_peak(t, n, me).wait_recv()
-
                 @pl.when(s == 0)
                 def _():
-                    wait(0)
+                    share_peak(t, 0, me).wait_recv()
 
                 @pl.when(s + 1 < slabs)
                 def _():
-                    wait(last)
+                    share_peak(t, last, me).wait_recv()
 
         for t in range(2):
             peak_in(t)
         factor = 2.0 / group_scale(s - 1, 3)
+        wide = group_ref[:, pl.ds(pl.multiple_of(s * SLAB, SLAB), SLAB)] == iota((GROUPS, SLAB), 0)
+        natural_ref[...] = jnp.max(jnp.where(wide, factor, 0.0), axis=0, keepdims=True)
+        wide = planar_group[pl.ds(s, 1), :] == iota((GROUPS, OCT * LANES), 0).astype(jnp.float32)
+        factor_ref[...] = jnp.max(jnp.where(wide, factor, 0.0), axis=0, keepdims=True)
+
+    def lattice(s, kk):
         at_slab = pl.ds(pl.multiple_of(s * SLAB, SLAB), SLAB)
-        wide = group_ref[:, at_slab] == iota((GROUPS, SLAB), 0)
-        natural = jnp.max(jnp.where(wide, factor, 0.0), axis=0, keepdims=True)
-        wide = planar_group[s] == iota((GROUPS, OCT * LANES), 0).astype(jnp.float32)
-        planar = jnp.max(jnp.where(wide, factor, 0.0), axis=0, keepdims=True)
-        scales = [planar[:, c * LANES:(c + 1) * LANES] for c in range(OCT)]
         octets = SLAB // OCT
         lane = iota((SUB, LANES), 1)
         place = s % PACK
-        here = lane // octets == place
+        inside = lane // octets == place
         at_error = pl.ds(pl.multiple_of(s // PACK * LANES, LANES), LANES)
-
-        def part(kk):
-            @pl.when(jnp.logical_not(is_hub))
-            def _():
-                for g in range(PACK):
-                    from_hub(s, kk * PACK + g, slot).wait_recv()
-
-            both = jnp.concatenate([cols[s, kk * PACK + g, hub_slot] for g in range(PACK)], axis=1)
-            planar_ref[...] = jnp.dot(both, p_ref[...], preferred_element_type=jnp.float32)
-
-            def tile(j):
-                at = pl.ds(pl.multiple_of(j * SUB, SUB), SUB)
-                for g in range(PACK):
-                    value = cols[s, kk * PACK + g, hub_slot, at, :].astype(jnp.float32) * natural
-                    scaled_ref[j, kk * PACK + g, :, at_slab] = value.astype(jnp.bfloat16)
-                square = near_sum = low = size = most = least = None
-                for c in range(OCT):
-                    value = planar_ref[at, c * LANES:(c + 1) * LANES] * scales[c]
-                    nearest = jnp.round(value)
-                    offset = jnp.abs(value - nearest)
-                    below = jnp.floor(value)
-                    if c == 0:
-                        square, near_sum, low, size = offset * offset, nearest, below, offset
-                        most = least = offset
-                    else:
-                        square, near_sum, low = square + offset * offset, near_sum + nearest, low + below
-                        size = size + offset
-                        most, least = jnp.maximum(most, offset), jnp.minimum(least, offset)
-                odd = near_sum - 2.0 * jnp.floor(near_sum * 0.5) > 0.5
-                whole = jnp.where(odd, square + (1.0 - 2.0 * most), square)
-                shifted = square + (OCT * 0.25 - size)
-                odd = low - 2.0 * jnp.floor(low * 0.5) > 0.5
-                error = jnp.minimum(whole, jnp.where(odd, shifted + 2.0 * least, shifted))
-                row = me * (blocks * HB) + j * HB + (kk * PACK + lane // octets) * SUB + iota((SUB, LANES), 0)
-                weight = (1.0 + 4.0 * (row.astype(jnp.float32) + 0.5) / total_rows) / 3.0
-                sum_ref[...] += error * weight
-                for g in range(PACK):
-                    turned = pltpu.roll(error, lax.rem(place + PACK - g, PACK) * octets, 1)
-                    old = error_ref[j, kk * PACK + g, :, at_error]
-                    error_ref[j, kk * PACK + g, :, at_error] = jnp.where(here, turned, old)
-
-            loop(blocks, tile)
-
-        loop(FOLD // PACK, part)
+        first = (me * (blocks * HB) + (kk * PACK + lane // octets) * SUB + iota((SUB, LANES), 0)).astype(jnp.float32)
+
+        @pl.when(jnp.logical_not(is_hub))
+        def _():
+            for g in range(PACK):
+                from_hub(s, kk * PACK + g, slot).wait_recv()
+
+        both = jnp.concatenate([cols[s, kk * PACK + g, hub_slot] for g in range(PACK)], axis=1)
+        planar_ref[...] = jnp.dot(both, p_ref[...], preferred_element_type=jnp.float32)
+
+        def tile(j):
+            at = pl.ds(pl.multiple_of(j * SUB, SUB), SUB)
+            natural = natural_ref[...]
+            for g in range(PACK):
+                value = cols[s, kk * PACK + g, hub_slot, at, :].astype(jnp.float32) * natural
+                scaled_ref[j, kk * PACK + g, :, at_slab] = value.astype(jnp.bfloat16)
+            square = near_sum = low = size = most = least = None
+            for c in range(OCT):
+                value = planar_ref[at, c * LANES:(c + 1) * LANES] * factor_ref[:, c * LANES:(c + 1) * LANES]
+                nearest = jnp.round(value)
+                offset = jnp.abs(value - nearest)
+                below = jnp.floor(value)
+                if c == 0:
+                    square, near_sum, low, size = offset * offset, nearest, below, offset
+                    most = least = offset
+                else:
+                    square, near_sum, low = square + offset * offset, near_sum + nearest, low + below
+                    size = size + offset
+                    most, least = jnp.maximum(most, offset), jnp.minimum(least, offset)
+            odd = near_sum - 2.0 * jnp.floor(near_sum * 0.5) > 0.5
+            whole = jnp.where(odd, square + (1.0 - 2.0 * most), square)
+            shifted = square + (OCT * 0.25 - size)
+            odd = low - 2.0 * jnp.floor(low * 0.5) > 0.5
+            error = jnp.minimum(whole, jnp.where(odd, shifted + 2.0 * least, shifted))
+            for g in range(PACK):
+                turned = pltpu.roll(error, lax.rem(place + PACK - g, PACK) * octets, 1)
+                old = error_ref[j, kk * PACK + g, :, at_error]
+                error_ref[j, kk * PACK + g, :, at_error] = jnp.where(inside, turned, old)
+            row = first + (j * HB).astype(jnp.float32)
+            return error * ((1.0 + 4.0 * (row + 0.5) / total_rows) / 3.0)
+
+        def some(i):
+            parts = [tile(i * unroll + u) for u in range(unroll)]
+            sum_ref[...] += sum(parts[1:], parts[0])
+
+        loop(blocks // unroll, some)
 
     column_side(0)
-    pl.semaphore_wait(barrier, peers + experts - 2)
+    pl.semaphore_wait(barrier, devices - 1)
 
     @pl.when(jnp.logical_not(is_hub))
     def _():
@@ -366,43 +361,58 @@
         loop(pairs - 1, step)
         loop(slabs - pairs, lambda q: send_slab(q + pairs))
 
+    for load in loads[3:]:
+        load.wait()
+
     @pl.when(is_hub)
     def _():
-        expand(gather_ref[side], gather, True)
-        expand(near_ref[side], near, True)
-        expand(spread_ref[side], spread, False)
-        loop(FOLD, lambda k: forward(0, k))
+        loop(LEAD, lambda k: forward(0, k))
 
     build_order(p_ref)
     sum_ref[...] = jnp.zeros_like(sum_ref)
-
-    def group_order(s):
-        row = group_ref[:, pl.ds(pl.multiple_of(s * SLAB, SLAB), SLAB)].astype(jnp.float32)
-        row = jnp.concatenate([jnp.broadcast_to(row, (SUB, SLAB)).astype(jnp.bfloat16)] * PACK, axis=1)
-        planar_group[s] = jnp.dot(row, p_ref[...], preferred_element_type=jnp.float32)[:1]
-
-    loop(slabs, group_order)
+    row = jnp.concatenate([group_ref[:, s * SLAB:(s + 1) * SLAB] for s in range(slabs)], axis=0)
+    row = jnp.concatenate([row.astype(jnp.float32).astype(jnp.bfloat16)] * PACK, axis=1)
+    planar_group[...] = jnp.dot(row, p_ref[...], preferred_element_type=jnp.float32)
 
     def stage(t):
+        mixes = jnp.logical_and(is_hub, t < slabs)
+
+        @pl.when(mixes)
+        def _():
+            peak_ref[...] = jnp.zeros_like(peak_ref)
+
         @pl.when(jnp.logical_and(is_hub, t + 1 < pairs))
         def _():
             column_side(t + 1)
 
-        @pl.when(t >= 2)
+        def part(kk):
+            @pl.when(mixes)
+            def _():
+                def step(i):
+                    k = kk * PACK + i
+                    ahead = t * FOLD + k + LEAD
+
+                    @pl.when(ahead < slabs * FOLD)
+                    def _():
+                        forward(ahead // FOLD, ahead % FOLD)
+
+                    backward(t, k)
+
+                loop(PACK, step)
+
+            @pl.when(t >= 2)
+            def _():
+                @pl.when(kk == 0)
+                def _():
+                    scale_slab(t - 2)
+
+                lattice(t - 2, kk)
+
+        loop(FOLD // PACK, part)
+
+        @pl.when(mixes)
         def _():
-            lattice(t - 2)
-
-        @pl.when(jnp.logical_and(is_hub, t < slabs))
-        def _():
-            def step(k, peak):
-                @pl.when(t + 1 < slabs)
-                def _():
-                    forward(t + 1, k)
-
-                return backward(t, k, peak)
-
-            peak = lax.fori_loop(0, FOLD, step, jnp.zeros((8, SLAB), jnp.float32))
-            peaks[side, t] = jnp.broadcast_to(jnp.max(peak, axis=0, keepdims=True), (8, SLAB))
+            peaks[side, t] = jnp.broadcast_to(jnp.max(peak_ref[...], axis=0, keepdims=True), (8, SLAB))
             for peer in others:
                 share_peak(side, t, peer).start()
 
@@ -412,22 +422,16 @@
     scale_ref[...] = jnp.broadcast_to(peak, (GROUPS, LANES)).T[:1, :GROUPS]
 
     part = jnp.sum(jnp.sum(sum_ref[...], axis=0, keepdims=True), axis=1, keepdims=True)
-    row_sums[me] = jnp.broadcast_to(part / (total_rows * width // OCT), (8, LANES))
-    for peer in others:
-        copy4(peer, me).start()
-    for peer in others:
-        copy4(peer, peer).wait_recv()
-    mean = row_sums[0]
-    for q in range(1, peers):
-        mean = mean + row_sums[q]
-    expert_sums[mine] = mean
-    for peer in elsewhere:
-        copy5(peer, mine).start()
-    for peer in elsewhere:
-        copy5(peer, peer).wait_recv()
-    total = expert_sums[0]
-    for e in range(1, experts):
-        total = total + expert_sums[e]
+    sums[here] = jnp.broadcast_to(part / (total_rows * width // OCT), (1, LANES))
+    loop(devices - 1, lambda n: share_sum(n + 1, here).start())
+
+    def wait_sum(n):
+        land = lax.rem(here + n + 1, devices)
+        share_sum(n + 1, land).wait_recv()
+
+    loop(devices - 1, wait_sum)
+    total = jnp.sum(sums[...], axis=0)
+    mean = jnp.sum(sums[pl.ds(mine * peers, peers)], axis=0)
     mean_ref[0] = jnp.max(mean)
     total_ref[0] = jnp.max(total / experts)
 
@@ -450,10 +454,7 @@
 
         loop(slabs, drain)
 
-    for peer in others:
-        copy4(peer, me).wait_send()
-    for peer in elsewhere:
-        copy5(peer, mine).wait_send()
+    loop(devices - 1, lambda n: share_sum(n + 1, here).wait_send())
 
 
 def put_kernel(scaled_ref, error_ref, scaled_out, error_out, sems):
@@ -491,7 +492,7 @@
     rows = blocks * SUB
     slabs = width // SLAB
     near, gather, spread = row_tables(BLOCKS)
-    inner, reach = mates * rows, gather.shape[1] * SUB
+    inner, reach = mates * rows, gather.shape[1]
     vmem = pl.BlockSpec(memory_space=pltpu.VMEM)
     hbm = pl.BlockSpec(memory_space=pl.ANY)
     dma = pltpu.SemaphoreType.DMA
@@ -505,25 +506,30 @@
             jax.ShapeDtypeStruct((1,), jnp.float32),
             jax.ShapeDtypeStruct((1,), jnp.float32),
         ),
-        in_specs=[hbm] + [vmem] * 6,
+        in_specs=[hbm] * 7,
         out_specs=(vmem, vmem, vmem, smem, smem),
         scratch_shapes=[
             pltpu.VMEM((blocks, HB, width), jnp.bfloat16),
-            pltpu.VMEM((blocks, HB, LANES), jnp.float32),
-            pltpu.VMEM((2, slabs // 2, half, SLAB), jnp.bfloat16),
+            pltpu.VMEM((1, local_rows), jnp.int32),
+            pltpu.VMEM((1, width), jnp.int32),
+            pltpu.VMEM((1, width), jnp.int32),
             pltpu.VMEM((inner, inner), jnp.bfloat16),
             pltpu.VMEM((reach, inner), jnp.bfloat16),
             pltpu.VMEM((inner, reach), jnp.bfloat16),
+            pltpu.VMEM((blocks, HB, LANES), jnp.float32),
+            pltpu.VMEM((2, slabs // 2, half, SLAB), jnp.bfloat16),
             pltpu.VMEM((PACK * SLAB, OCT * LANES), jnp.bfloat16),
             pltpu.VMEM((slabs, FOLD, mates, rows, SLAB), jnp.bfloat16),
             pltpu.VMEM((slabs, FOLD, reach, SLAB), jnp.bfloat16),
             pltpu.VMEM((slabs, FOLD, reach, SLAB), jnp.bfloat16),
             pltpu.VMEM((rows, OCT * LANES), jnp.float32),
-            pltpu.VMEM((slabs, 1, OCT * LANES), jnp.float32),
+            pltpu.VMEM((slabs, OCT * LANES), jnp.float32),
             pltpu.VMEM((2, slabs, 8, SLAB), jnp.float32),
+            pltpu.VMEM((8, SLAB), jnp.float32),
+            pltpu.VMEM((1, SLAB), jnp.float32),
+            pltpu.VMEM((1, OCT * LANES), jnp.float32),
             pltpu.VMEM((SUB, LANES), jnp.float32),
-            pltpu.VMEM((peers, 8, LANES), jnp.float32),
-            pltpu.VMEM((experts, 8, LANES), jnp.float32),
+            pltpu.VMEM((peers * experts, 1, LANES), jnp.float32),
             dma((slabs, FOLD)),
             dma((slabs, FOLD, mates)),
             dma((slabs, FOLD, mates)),
@@ -532,11 +538,9 @@
             dma((2, slabs)),
             dma((slabs, FOLD)),
             dma((slabs, FOLD)),
-            dma((peers,)),
-            dma((peers,)),
-            dma((experts,)),
-            dma((experts,)),
-            dma,
+            dma((peers * experts,)),
+            dma((peers * experts,)),
+            dma((7,)),
         ],
         compiler_params=pltpu.CompilerParams(
             collective_id=0, has_side_effects=True, vmem_limit_bytes=54 * 2**20

time: 319 us -> 279 us (0.87)
  Pallas kernels: 314 us -> 274 us
    pallas_call x1, Pallas kernels: 311 us -> 270 us  [body(): pl.pallas_call(functools.partial(kernel, peers, experts), out_shape=(pltp...]
where the time goes in v2:
time: 279 us
  Pallas kernels  274 us (98%)
  between operations  4.15 us (1%)
    pallas_call x1, Pallas kernels, body(): pl.pallas_call(functools.partial(kernel, peers, experts), out_shape=(pltp...  270 us

profile of v2, /device:TPU:0, one launch (start us, length us, event | category | flops | bytes accessed | tf_op | source)
XLA Modules:
  0.0 278.6 jit_solution(8368364267587669867)
XLA Ops:
  0.6 270.3 %shard_map.110 = (bf16[14,8,16,2048]{3,2,1,0:T(8,128)(2,1)S(1)}, f32[14,8,16,256]{3,2,1,0:T(8,128)S(1)}, f32[1,16]{1,0:T(1,128)}, f32[1]{0:T(128)}, f32[1]{0:T(128)}) custom-call(bf16[14,128,2048]{2,1,0:T(8,128)(2,1)} %bitcast.4, s32[1,1792]{1,0:T(1,128)} %left_hbm.1, s32[1,2048]{1,0:T(1,128)} %right_hbm.1, s32[1,2048]{1,0:T(1,128)} %group_hbm.1, ...), custom_call_target="tpu_custom_call" | custom-call | tf_op jit(solution)/shard_map/pallas_call | solution.py:500
  271.0 0.0 copy-start
  271.0 3.7 %shard_map.111 = (bf16[14,8,16,2048]{3,2,1,0:T(8,128)(2,1)}, f32[14,8,16,256]{3,2,1,0:T(8,128)}) custom-call(bf16[14,8,16,2048]{3,2,1,0:T(8,128)(2,1)S(1)} %get-tuple-element.12.scaled_ref, f32[14,8,16,256]{3,2,1,0:T(8,128)S(1)} %get-tuple-element.13.error_ref), custom_call_target="tpu_custom_call" | custom-call | tf_op jit(solution)/shard_map/pallas_call | solution.py:472
  274.6 0.0 copy-done
  274.6 0.5 copy.15
Async XLA Ops:
  271.0 3.7 %copy-start = (f32[1,16]{1,0:T(1,128)S(1)}, f32[1,16]{1,0:T(1,128)}, u32[]{:S(2)}) copy-start(f32[1,16]{1,0:T(1,128)} %get-tuple-element.26) | copy-start | bytes 196

commit v3 on v2

--- a/solution.py
+++ b/solution.py
@@ -179,6 +179,9 @@
     here = mine * peers + me
     mate_slots = [lax.rem(hub_slot + d, mates) for d in range(1, mates)]
 
+    def who_index(who):
+        return jnp.where(who > hub_slot, who - 1, who)
+
     def remote(src, dst, send_sem, recv_sem, peer):
         return pltpu.make_async_remote_copy(
             src_ref=src, dst_ref=dst, send_sem=send_sem, recv_sem=recv_sem,
@@ -187,37 +190,63 @@
 
     def to_hub(s, k, who):
         piece = cols.at[s, k, who]
-        return remote(piece, piece, send1.at[s, k], recv1.at[s, k, who], hub)
+        return remote(piece, piece, send1.at[s], recv1.at[s, k, who_index(who)], hub)
+
+    def all_to_hub(s):
+        piece = cols.at[s, :, slot]
+        return remote(piece, piece, send1.at[s], recv1.at[s, 0, 0], hub)
 
     def from_hub(s, k, who):
         return remote(
-            cols.at[s, k, who], cols.at[s, k, hub_slot], send2.at[s, k, who], recv2.at[s, k],
+            cols.at[s, k, who], cols.at[s, k, hub_slot], send2.at[s, who_index(who)], recv2.at[s, k // PACK],
             side * mates + who,
         )
 
+    def all_from_hub(s, who):
+        piece = cols.at[s, :, who]
+        return remote(piece, piece, send2.at[s, who_index(who)], recv2.at[s, 0], side * mates + who)
+
+    def four_from_hub(s, kk):
+        piece = cols.at[s, pl.ds(kk * PACK, PACK), hub_slot]
+        return remote(piece, piece, send2.at[s, 0], recv2.at[s, kk], hub)
+
     def across(s, k):
-        return remote(out_s.at[s, k], in_s.at[s, k], send_s.at[s, k], recv_s.at[s, k], far_hub)
+        return remote(out_s.at[s, k], in_s.at[s, k], send_s.at[s], recv_s.at[s, k], far_hub)
+
+    def all_across(s):
+        return remote(out_s.at[s], in_s.at[s], send_s.at[s], recv_s.at[s, 0], far_hub)
 
     def share_peak(t, s, peer):
         piece = peaks.at[t, s]
-        return remote(piece, piece, send3.at[s, peer], recv3.at[t, s], peer)
-
-    def share_sum(n, land):
-        there = lax.rem(here + n, devices)
+        return remote(piece, piece, send3.at[peer], recv3.at[t, s], peer)
+
+    def all_peaks(peer):
+        return remote(peaks.at[side], peaks.at[side], send3.at[peer], recv3.at[0, 0], peer)
+
+    def wrap(value, bound):
+        return jnp.where(value >= bound, value - bound, value)
+
+    places = [
+        {"expert": wrap(mine + e, experts), "row": wrap(me + r, peers)}
+        for e in range(experts) for r in range(peers) if e + r
+    ]
+
+    def share_sum(place):
+        piece = sums.at[here]
         return pltpu.make_async_remote_copy(
-            src_ref=sums.at[here], dst_ref=sums.at[land], send_sem=send4.at[there], recv_sem=recv4.at[land],
-            device_id={"expert": there // peers, "row": lax.rem(there, peers)}, device_id_type=MESH,
+            src_ref=piece, dst_ref=piece, send_sem=send4, recv_sem=recv4, device_id=place, device_id_type=MESH
         )
 
+    def all_sums():
+        piece = sums.at[pl.ds(0, devices - 1)]
+        return pltpu.make_async_remote_copy(
+            src_ref=piece, dst_ref=piece, send_sem=send4, recv_sem=recv4, device_id=places[0], device_id_type=MESH
+        )
+
     barrier = pltpu.get_barrier_semaphore()
 
-    def greet(n):
-        there = lax.rem(here + n + 1, devices)
-        pl.semaphore_signal(
-            barrier, inc=1, device_id={"expert": there // peers, "row": lax.rem(there, peers)}, device_id_type=MESH
-        )
-
-    loop(devices - 1, greet)
+    for place in places:
+        pl.semaphore_signal(barrier, inc=1, device_id=place, device_id_type=MESH)
     loads[0].wait()
     build_column(right_ref, h_ref, 1.0 / math.sqrt(width * HB))
     loads[1].wait()
@@ -254,9 +283,16 @@
         r = jnp.dot(near[...], z, preferred_element_type=jnp.float32)
         r = r + jnp.dot(spread[...], in_s[s, k], preferred_element_type=jnp.float32)
         cols[s, k] = r.astype(jnp.bfloat16).reshape(mates, rows, SLAB)
+        peak_ref[...] = jnp.maximum(peak_ref[...], jnp.max(jnp.abs(r).reshape(-1, 8, SLAB), axis=0))
+
+        @pl.when(k == FOLD - 1)
+        def _():
+            peaks[side, s] = jnp.broadcast_to(jnp.max(peak_ref[...], axis=0, keepdims=True), (8, SLAB))
+            for peer in others:
+                share_peak(side, s, peer).start()
+
         for who in mate_slots:
             from_hub(s, k, who).start()
-        peak_ref[...] = jnp.maximum(peak_ref[...], jnp.max(jnp.abs(r).reshape(-1, 8, SLAB), axis=0))
 
     def group_scale(first, count):
         span = count * SLAB
@@ -269,7 +305,7 @@
         return jnp.maximum(jnp.max(jnp.where(inside, top, 0.0), axis=1, keepdims=True), 1.0)
 
     total_rows = peers * blocks * HB
-    unroll = next(u for u in (2, 1) if blocks % u == 0)
+    unroll = next(u for u in (7, 1) if blocks % u == 0)
 
     def scale_slab(s):
         last = jnp.minimum(s + 1, slabs - 1)
@@ -292,6 +328,14 @@
         natural_ref[...] = jnp.max(jnp.where(wide, factor, 0.0), axis=0, keepdims=True)
         wide = planar_group[pl.ds(s, 1), :] == iota((GROUPS, OCT * LANES), 0).astype(jnp.float32)
         factor_ref[...] = jnp.max(jnp.where(wide, factor, 0.0), axis=0, keepdims=True)
+
+    def permute(s, kk):
+        @pl.when(jnp.logical_not(is_hub))
+        def _():
+            four_from_hub(s, kk).wait_recv()
+
+        both = jnp.concatenate([cols[s, kk * PACK + g, hub_slot] for g in range(PACK)], axis=1)
+        planar_ref[s % 2, kk] = jnp.dot(both, p_ref[...], preferred_element_type=jnp.float32)
 
     def lattice(s, kk):
         at_slab = pl.ds(pl.multiple_of(s * SLAB, SLAB), SLAB)
@@ -302,14 +346,6 @@
         at_error = pl.ds(pl.multiple_of(s // PACK * LANES, LANES), LANES)
         first = (me * (blocks * HB) + (kk * PACK + lane // octets) * SUB + iota((SUB, LANES), 0)).astype(jnp.float32)
 
-        @pl.when(jnp.logical_not(is_hub))
-        def _():
-            for g in range(PACK):
-                from_hub(s, kk * PACK + g, slot).wait_recv()
-
-        both = jnp.concatenate([cols[s, kk * PACK + g, hub_slot] for g in range(PACK)], axis=1)
-        planar_ref[...] = jnp.dot(both, p_ref[...], preferred_element_type=jnp.float32)
-
         def tile(j):
             at = pl.ds(pl.multiple_of(j * SUB, SUB), SUB)
             natural = natural_ref[...]
@@ -318,7 +354,7 @@
                 scaled_ref[j, kk * PACK + g, :, at_slab] = value.astype(jnp.bfloat16)
             square = near_sum = low = size = most = least = None
             for c in range(OCT):
-                value = planar_ref[at, c * LANES:(c + 1) * LANES] * factor_ref[:, c * LANES:(c + 1) * LANES]
+                value = planar_ref[s % 2, kk, at, c * LANES:(c + 1) * LANES] * factor_ref[:, c * LANES:(c + 1) * LANES]
                 nearest = jnp.round(value)
                 offset = jnp.abs(value - nearest)
                 below = jnp.floor(value)
@@ -408,13 +444,13 @@
 
                 lattice(t - 2, kk)
 
+            come = jnp.where(is_hub, t, t - kk)
+
+            @pl.when(jnp.logical_and(come >= 0, come < slabs))
+            def _():
+                permute(come, kk)
+
         loop(FOLD // PACK, part)
-
-        @pl.when(mixes)
-        def _():
-            peaks[side, t] = jnp.broadcast_to(jnp.max(peak_ref[...], axis=0, keepdims=True), (8, SLAB))
-            for peer in others:
-                share_peak(side, t, peer).start()
 
     loop(slabs + 2, stage)
 
@@ -423,13 +459,9 @@
 
     part = jnp.sum(jnp.sum(sum_ref[...], axis=0, keepdims=True), axis=1, keepdims=True)
     sums[here] = jnp.broadcast_to(part / (total_rows * width // OCT), (1, LANES))
-    loop(devices - 1, lambda n: share_sum(n + 1, here).start())
-
-    def wait_sum(n):
-        land = lax.rem(here + n + 1, devices)
-        share_sum(n + 1, land).wait_recv()
-
-    loop(devices - 1, wait_sum)
+    for place in places:
+        share_sum(place).start()
+    all_sums().wait_recv()
     total = jnp.sum(sums[...], axis=0)
     mean = jnp.sum(sums[pl.ds(mine * peers, peers)], axis=0)
     mean_ref[0] = jnp.max(mean)
@@ -437,24 +469,21 @@
 
     @pl.when(jnp.logical_not(is_hub))
     def _():
-        loop(slabs, lambda s: loop(FOLD, lambda k: to_hub(s, k, slot).wait_send()))
+        loop(slabs, lambda s: all_to_hub(s).wait_send())
 
     @pl.when(is_hub)
     def _():
+        for peer in others:
+            all_peaks(peer).wait_send()
+
         def drain(s):
-            for peer in others:
-                share_peak(side, s, peer).wait_send()
-
-            def step(k):
-                across(s, k).wait_send()
-                for who in mate_slots:
-                    from_hub(s, k, who).wait_send()
-
-            loop(FOLD, step)
+            all_across(s).wait_send()
+            for who in mate_slots:
+                all_from_hub(s, who).wait_send()
 
         loop(slabs, drain)
 
-    loop(devices - 1, lambda n: share_sum(n + 1, here).wait_send())
+    all_sums().wait_send()
 
 
 def put_kernel(scaled_ref, error_ref, scaled_out, error_out, sems):
@@ -522,7 +551,7 @@
             pltpu.VMEM((slabs, FOLD, mates, rows, SLAB), jnp.bfloat16),
             pltpu.VMEM((slabs, FOLD, reach, SLAB), jnp.bfloat16),
             pltpu.VMEM((slabs, FOLD, reach, SLAB), jnp.bfloat16),
-            pltpu.VMEM((rows, OCT * LANES), jnp.float32),
+            pltpu.VMEM((2, FOLD // PACK, rows, OCT * LANES), jnp.float32),
             pltpu.VMEM((slabs, OCT * LANES), jnp.float32),
             pltpu.VMEM((2, slabs, 8, SLAB), jnp.float32),
             pltpu.VMEM((8, SLAB), jnp.float32),
@@ -530,16 +559,16 @@
             pltpu.VMEM((1, OCT * LANES), jnp.float32),
             pltpu.VMEM((SUB, LANES), jnp.float32),
             pltpu.VMEM((peers * experts, 1, LANES), jnp.float32),
+            dma((slabs,)),
+            dma((slabs, FOLD, max(mates - 1, 1))),
+            dma((slabs, max(mates - 1, 1))),
+            dma((slabs, FOLD // PACK)),
+            dma((peers,)),
+            dma((2, slabs)),
+            dma((slabs,)),
             dma((slabs, FOLD)),
-            dma((slabs, FOLD, mates)),
-            dma((slabs, FOLD, mates)),
-            dma((slabs, FOLD)),
-            dma((slabs, peers)),
-            dma((2, slabs)),
-            dma((slabs, FOLD)),
-            dma((slabs, FOLD)),
-            dma((peers * experts,)),
-            dma((peers * experts,)),
+            dma,
+            dma,
             dma((7,)),
         ],
         compiler_params=pltpu.CompilerParams(

time: 279 us -> 269 us (0.964)
  Pallas kernels: 274 us -> 264 us
    pallas_call x1, Pallas kernels: 270 us -> 260 us  [body(): pl.pallas_call(functools.partial(kernel, peers, experts), out_shape=(pltp...]
where the time goes in v3:
time: 269 us
  Pallas kernels  264 us (98%)
  between operations  4.15 us (2%)
    pallas_call x1, Pallas kernels, body(): pl.pallas_call(functools.partial(kernel, peers, experts), out_shape=(pltp...  260 us

profile of v3, /device:TPU:0, one launch (start us, length us, event | category | flops | bytes accessed | tf_op | source)
XLA Modules:
  0.0 268.7 jit_solution(293075697454458693)
XLA Ops:
  0.6 260.4 %shard_map.110 = (bf16[14,8,16,2048]{3,2,1,0:T(8,128)(2,1)S(1)}, f32[14,8,16,256]{3,2,1,0:T(8,128)S(1)}, f32[1,16]{1,0:T(1,128)}, f32[1]{0:T(128)}, f32[1]{0:T(128)}) custom-call(bf16[14,128,2048]{2,1,0:T(8,128)(2,1)} %bitcast.4, s32[1,1792]{1,0:T(1,128)} %left_hbm.1, s32[1,2048]{1,0:T(1,128)} %right_hbm.1, s32[1,2048]{1,0:T(1,128)} %group_hbm.1, ...), custom_call_target="tpu_custom_call" | custom-call | tf_op jit(solution)/shard_map/pallas_call | solution.py:529
  261.0 0.0 copy-start
  261.0 3.7 %shard_map.111 = (bf16[14,8,16,2048]{3,2,1,0:T(8,128)(2,1)}, f32[14,8,16,256]{3,2,1,0:T(8,128)}) custom-call(bf16[14,8,16,2048]{3,2,1,0:T(8,128)(2,1)S(1)} %get-tuple-element.12.scaled_ref, f32[14,8,16,256]{3,2,1,0:T(8,128)S(1)} %get-tuple-element.13.error_ref), custom_call_target="tpu_custom_call" | custom-call | tf_op jit(solution)/shard_map/pallas_call | solution.py:501
  264.7 0.0 copy-done
  264.7 0.5 copy.15
Async XLA Ops:
  261.0 3.7 %copy-start = (f32[1,16]{1,0:T(1,128)S(1)}, f32[1,16]{1,0:T(1,128)}, u32[]{:S(2)}) copy-start(f32[1,16]{1,0:T(1,128)} %get-tuple-element.26) | copy-start | bytes 196

commit v4 on v3

--- a/solution.py
+++ b/solution.py
@@ -19,6 +19,7 @@
 SLAB = 256
 PACK = LANES * OCT // SLAB
 LEAD = 3
+EARLY = 5
 MESH = pl.DeviceIdType.MESH
 
 
@@ -44,37 +45,39 @@
     return np.where(first == 0.0, table * math.sqrt(0.5), table)
 
 
-def cross_factors(order, to):
+def cross_factors(order, to, own):
     half = order // 2
     block = cosine_table(order)[to * half:(to + 1) * half, (1 - to) * half:(2 - to) * half]
     even, odd = block[0::2], block[1::2]
     along = odd @ even.T / np.sum(even * even, axis=1)
-    u, s, v = np.linalg.svd(odd - along @ even)
+    _, s, v = np.linalg.svd(odd - along @ even)
     kept = int(np.sum(s > 2.0 ** -24))
-    v, u = v[:kept], u[:, :kept] * s[:kept]
-    flip = np.sign(np.take_along_axis(v, np.argmax(np.abs(v), axis=1)[:, None], axis=1))
-    count = even.shape[0]
-    gather = np.concatenate([even, v * flip])
-    spread = np.zeros((half, count + kept))
-    spread[0::2, :count] = np.eye(count)
-    spread[1::2, :count] = along
-    spread[1::2, count:] = u * flip[:, 0]
-    return gather, spread
-
-
-def row_tables(order):
+    basis = np.concatenate([even / np.sqrt(np.sum(even * even, axis=1, keepdims=True)), v[:kept]])
+    far = slice(0, half - own) if to else slice(own, half)
+    alone = max(0, basis.shape[0] - (half - own))
+    if alone:
+        turn = np.linalg.svd(basis[:, far].T)[2][::-1]
+        basis = turn @ basis
+        basis[:alone, far] = 0.0
+    return basis, block @ basis.T, alone
+
+
+def row_tables(order, own):
     half = order // 2
     table = cosine_table(order)
     near = np.stack([table[s * half:(s + 1) * half, s * half:(s + 1) * half] for s in range(2)])
-    to_low, to_high = cross_factors(order, 0), cross_factors(order, 1)
+    to_low, to_high = cross_factors(order, 0, own), cross_factors(order, 1, own)
     gather = np.stack([to_high[0], to_low[0]])
     spread = np.stack([to_low[1], to_high[1]])
     index = np.arange(SUB)
     inner = np.array([[1 - 2 * (bin(a & b).count("1") & 1) for b in index] for a in index], np.float32)
-    return tuple(
+    tables = [
         np.stack([np.kron(t, m) for t in ts]).astype(np.float32).astype(np.dtype(jnp.bfloat16))
         for ts, m in ((near, inner), (gather, inner), (spread, np.eye(SUB, dtype=np.float32)))
-    )
+    ]
+    alone = to_high[2] * SUB
+    first = np.stack([tables[1][0][:alone, (half - own) * SUB:], tables[1][1][:alone, :own * SUB]])
+    return tables, first
 
 
 def build_column(right_ref, h_ref, scale):
@@ -144,12 +147,12 @@
 
 
 def kernel(
-    peers, experts, x_hbm, left_hbm, right_hbm, group_hbm, near_hbm, gather_hbm, spread_hbm,
+    peers, experts, alone, x_hbm, left_hbm, right_hbm, group_hbm, near_hbm, gather_hbm, spread_hbm, first_hbm,
     scaled_ref, error_ref, scale_ref, mean_ref, total_ref,
-    x_ref, left_ref, right_ref, group_ref, near, gather, spread,
+    x_ref, left_ref, right_ref, group_ref, near, gather, spread, first,
     left, h_ref, p_ref, cols, out_s, in_s, planar_ref, planar_group, peaks, peak_ref, natural_ref, factor_ref,
     sum_ref, sums,
-    send1, recv1, send2, recv2, send3, recv3, send_s, recv_s, send4, recv4, load_sem,
+    send1, recv1, send2, recv2, send3, recv3, send_s, recv_s, recv_first, send4, recv4, load_sem,
 ):
     blocks, _, width = x_ref.shape
     half = width // 2
@@ -169,7 +172,7 @@
         pltpu.make_async_copy(src, dst, load_sem.at[n])
         for n, (src, dst) in enumerate((
             (right_hbm, right_ref), (left_hbm, left_ref), (x_hbm, x_ref), (group_hbm, group_ref),
-            (gather_hbm.at[side], gather), (near_hbm.at[side], near), (spread_hbm.at[side], spread),
+            (first_hbm.at[side], first), (gather_hbm.at[side], gather), (near_hbm.at[side], near), (spread_hbm.at[side], spread),
         ))
     ]
     for load in loads:
@@ -213,6 +216,13 @@
     def across(s, k):
         return remote(out_s.at[s, k], in_s.at[s, k], send_s.at[s], recv_s.at[s, k], far_hub)
 
+    def across_part(k, low):
+        at = pl.ds(0, alone) if low else pl.ds(alone, gather.shape[0] - alone)
+        return remote(
+            out_s.at[0, k, at], in_s.at[0, k, at], send_s.at[0],
+            recv_first.at[k] if low else recv_s.at[0, k], far_hub,
+        )
+
     def all_across(s):
         return remote(out_s.at[s], in_s.at[s], send_s.at[s], recv_s.at[s, 0], far_hub)
 
@@ -226,10 +236,16 @@
     def wrap(value, bound):
         return jnp.where(value >= bound, value - bound, value)
 
-    places = [
-        {"expert": wrap(mine + e, experts), "row": wrap(me + r, peers)}
-        for e in range(experts) for r in range(peers) if e + r
-    ]
+    def each_other(act):
+        def step(e):
+            for r in range(peers):
+                place = {"expert": wrap(mine + e, experts), "row": wrap(me + r, peers)}
+                if r:
+                    act(place)
+                else:
+                    pl.when(e > 0)(lambda: act(place))
+
+        loop(experts, step)
 
     def share_sum(place):
         piece = sums.at[here]
@@ -240,13 +256,13 @@
     def all_sums():
         piece = sums.at[pl.ds(0, devices - 1)]
         return pltpu.make_async_remote_copy(
-            src_ref=piece, dst_ref=piece, send_sem=send4, recv_sem=recv4, device_id=places[0], device_id_type=MESH
+            src_ref=piece, dst_ref=piece, send_sem=send4, recv_sem=recv4, device_id={"row": others[0]},
+            device_id_type=MESH,
         )
 
     barrier = pltpu.get_barrier_semaphore()
 
-    for place in places:
-        pl.semaphore_signal(barrier, inc=1, device_id=place, device_id_type=MESH)
+    each_other(lambda place: pl.semaphore_signal(barrier, inc=1, device_id=place, device_id_type=MESH))
     loads[0].wait()
     build_column(right_ref, h_ref, 1.0 / math.sqrt(width * HB))
     loads[1].wait()
@@ -272,13 +288,43 @@
     def forward(s, k):
         for who in mate_slots:
             to_hub(s, k, who).wait_recv()
-        z = cols[s, k].reshape(mates * rows, SLAB)
-        r = jnp.dot(gather[...], z, preferred_element_type=jnp.float32)
-        out_s[s, k] = r.astype(jnp.bfloat16)
-        across(s, k).start()
+
+        def full():
+            z = cols[s, k].reshape(mates * rows, SLAB)
+            r = jnp.dot(gather[...], z, preferred_element_type=jnp.float32)
+            out_s[s, k] = r.astype(jnp.bfloat16)
+            across(s, k).start()
+
+        def remainder():
+            z = cols[0, k].reshape(mates * rows, SLAB)
+            r = jnp.dot(gather[alone:, :], z, preferred_element_type=jnp.float32)
+            out_s[0, k, alone:, :] = r.astype(jnp.bfloat16)
+            across_part(k, False).start()
+
+        if early:
+            begun = jnp.logical_and(s == 0, k < early)
+            pl.when(begun)(remainder)
+            pl.when(jnp.logical_not(begun))(full)
+        else:
+            full()
+
+    def forward_alone(k):
+        r = jnp.dot(first[...], cols[0, k, hub_slot], preferred_element_type=jnp.float32)
+        out_s[0, k, :alone, :] = r.astype(jnp.bfloat16)
+        across_part(k, True).start()
 
     def backward(s, k):
-        across(s, k).wait_recv()
+        if early:
+            begun = jnp.logical_and(s == 0, k < early)
+
+            @pl.when(begun)
+            def _():
+                across_part(k, True).wait_recv()
+                across_part(k, False).wait_recv()
+
+            pl.when(jnp.logical_not(begun))(lambda: across(s, k).wait_recv())
+        else:
+            across(s, k).wait_recv()
         z = cols[s, k].reshape(mates * rows, SLAB)
         r = jnp.dot(near[...], z, preferred_element_type=jnp.float32)
         r = r + jnp.dot(spread[...], in_s[s, k], preferred_element_type=jnp.float32)
@@ -305,6 +351,7 @@
         return jnp.maximum(jnp.max(jnp.where(inside, top, 0.0), axis=1, keepdims=True), 1.0)
 
     total_rows = peers * blocks * HB
+    early = EARLY if alone else 0
     unroll = next(u for u in (7, 1) if blocks % u == 0)
 
     def scale_slab(s):
@@ -325,7 +372,7 @@
             peak_in(t)
         factor = 2.0 / group_scale(s - 1, 3)
         wide = group_ref[:, pl.ds(pl.multiple_of(s * SLAB, SLAB), SLAB)] == iota((GROUPS, SLAB), 0)
-        natural_ref[...] = jnp.max(jnp.where(wide, factor, 0.0), axis=0, keepdims=True)
+        natural_ref[pl.ds(s % 2, 1), :] = jnp.max(jnp.where(wide, factor, 0.0), axis=0, keepdims=True)
         wide = planar_group[pl.ds(s, 1), :] == iota((GROUPS, OCT * LANES), 0).astype(jnp.float32)
         factor_ref[...] = jnp.max(jnp.where(wide, factor, 0.0), axis=0, keepdims=True)
 
@@ -337,8 +384,23 @@
         both = jnp.concatenate([cols[s, kk * PACK + g, hub_slot] for g in range(PACK)], axis=1)
         planar_ref[s % 2, kk] = jnp.dot(both, p_ref[...], preferred_element_type=jnp.float32)
 
+    def write_scaled(s, kk):
+        at_slab = pl.ds(pl.multiple_of(s * SLAB, SLAB), SLAB)
+        natural = natural_ref[pl.ds(s % 2, 1), :]
+
+        def tile(j):
+            at = pl.ds(pl.multiple_of(j * SUB, SUB), SUB)
+            for g in range(PACK):
+                value = cols[s, kk * PACK + g, hub_slot, at, :].astype(jnp.float32) * natural
+                scaled_ref[j, kk * PACK + g, :, at_slab] = value.astype(jnp.bfloat16)
+
+        def some(i):
+            for u in range(unroll):
+                tile(i * unroll + u)
+
+        loop(blocks // unroll, some)
+
     def lattice(s, kk):
-        at_slab = pl.ds(pl.multiple_of(s * SLAB, SLAB), SLAB)
         octets = SLAB // OCT
         lane = iota((SUB, LANES), 1)
         place = s % PACK
@@ -348,10 +410,6 @@
 
         def tile(j):
             at = pl.ds(pl.multiple_of(j * SUB, SUB), SUB)
-            natural = natural_ref[...]
-            for g in range(PACK):
-                value = cols[s, kk * PACK + g, hub_slot, at, :].astype(jnp.float32) * natural
-                scaled_ref[j, kk * PACK + g, :, at_slab] = value.astype(jnp.bfloat16)
             square = near_sum = low = size = most = least = None
             for c in range(OCT):
                 value = planar_ref[s % 2, kk, at, c * LANES:(c + 1) * LANES] * factor_ref[:, c * LANES:(c + 1) * LANES]
@@ -402,6 +460,8 @@
 
     @pl.when(is_hub)
     def _():
+        if early:
+            loop(early, forward_alone)
         loop(LEAD, lambda k: forward(0, k))
 
     build_order(p_ref)
@@ -443,6 +503,7 @@
                     scale_slab(t - 2)
 
                 lattice(t - 2, kk)
+                pl.when(t < slabs)(lambda: write_scaled(t - 2, kk))
 
             come = jnp.where(is_hub, t, t - kk)
 
@@ -459,8 +520,9 @@
 
     part = jnp.sum(jnp.sum(sum_ref[...], axis=0, keepdims=True), axis=1, keepdims=True)
     sums[here] = jnp.broadcast_to(part / (total_rows * width // OCT), (1, LANES))
-    for place in places:
-        share_sum(place).start()
+    each_other(lambda place: share_sum(place).start())
+    loop(FOLD // PACK, lambda kk: write_scaled(slabs - 2, kk))
+    loop(FOLD // PACK, lambda kk: write_scaled(slabs - 1, kk))
     all_sums().wait_recv()
     total = jnp.sum(sums[...], axis=0)
     mean = jnp.sum(sums[pl.ds(mine * peers, peers)], axis=0)
@@ -520,14 +582,16 @@
     mates = peers // 2
     rows = blocks * SUB
     slabs = width // SLAB
-    near, gather, spread = row_tables(BLOCKS)
+    (near, gather, spread), first = row_tables(BLOCKS, blocks)
+    alone = first.shape[1]
+    first = first if alone else gather
     inner, reach = mates * rows, gather.shape[1]
     vmem = pl.BlockSpec(memory_space=pltpu.VMEM)
     hbm = pl.BlockSpec(memory_space=pl.ANY)
     dma = pltpu.SemaphoreType.DMA
     smem = pl.BlockSpec(memory_space=pltpu.SMEM)
     scaled, errors, group_scale, mean, total = pl.pallas_call(
-        functools.partial(kernel, peers, experts),
+        functools.partial(kernel, peers, experts, alone),
         out_shape=(
             pltpu.VMEM((blocks, FOLD, SUB, width), jnp.bfloat16),
             pltpu.VMEM((blocks, FOLD, SUB, width // OCT), jnp.float32),
@@ -535,7 +599,7 @@
             jax.ShapeDtypeStruct((1,), jnp.float32),
             jax.ShapeDtypeStruct((1,), jnp.float32),
         ),
-        in_specs=[hbm] * 7,
+        in_specs=[hbm] * 8,
         out_specs=(vmem, vmem, vmem, smem, smem),
         scratch_shapes=[
             pltpu.VMEM((blocks, HB, width), jnp.bfloat16),
@@ -545,6 +609,7 @@
             pltpu.VMEM((inner, inner), jnp.bfloat16),
             pltpu.VMEM((reach, inner), jnp.bfloat16),
             pltpu.VMEM((inner, reach), jnp.bfloat16),
+            pltpu.VMEM(first.shape[1:], jnp.bfloat16),
             pltpu.VMEM((blocks, HB, LANES), jnp.float32),
             pltpu.VMEM((2, slabs // 2, half, SLAB), jnp.bfloat16),
             pltpu.VMEM((PACK * SLAB, OCT * LANES), jnp.bfloat16),
@@ -555,7 +620,7 @@
             pltpu.VMEM((slabs, OCT * LANES), jnp.float32),
             pltpu.VMEM((2, slabs, 8, SLAB), jnp.float32),
             pltpu.VMEM((8, SLAB), jnp.float32),
-            pltpu.VMEM((1, SLAB), jnp.float32),
+            pltpu.VMEM((2, SLAB), jnp.float32),
             pltpu.VMEM((1, OCT * LANES), jnp.float32),
             pltpu.VMEM((SUB, LANES), jnp.float32),
             pltpu.VMEM((peers * experts, 1, LANES), jnp.float32),
@@ -567,14 +632,15 @@
             dma((2, slabs)),
             dma((slabs,)),
             dma((slabs, FOLD)),
+            dma((EARLY,)),
             dma,
             dma,
-            dma((7,)),
+            dma((8,)),
         ],
         compiler_params=pltpu.CompilerParams(
             collective_id=0, has_side_effects=True, vmem_limit_bytes=54 * 2**20
         ),
-    )(weights.reshape(blocks, HB, width), left_bits, right_bits, groups, near, gather, spread)
+    )(weights.reshape(blocks, HB, width), left_bits, right_bits, groups, near, gather, spread, first)
     scaled, errors = put(scaled, errors)
     return (
         scaled.reshape(1, local_rows, width),

time: 269 us -> 267 us (level)
  no operation moved by 1% of the time
where the time goes in v4:
time: 267 us; the launch traced here: 266 us
  Pallas kernels  262 us (98%)
  between operations  4.15 us (2%)
    pallas_call x1, Pallas kernels, body(): pl.pallas_call(functools.partial(kernel, peers, experts, alone), out_shap...  258 us

profile of v4, /device:TPU:0, one launch (start us, length us, event | category | flops | bytes accessed | tf_op | source)
XLA Modules:
  0.0 266.3 jit_solution(12789203307453758837)
XLA Ops:
  0.6 258.0 %shard_map.119 = (bf16[14,8,16,2048]{3,2,1,0:T(8,128)(2,1)S(1)}, f32[14,8,16,256]{3,2,1,0:T(8,128)S(1)}, f32[1,16]{1,0:T(1,128)}, f32[1]{0:T(128)}, f32[1]{0:T(128)}) custom-call(bf16[14,128,2048]{2,1,0:T(8,128)(2,1)} %bitcast.4, s32[1,1792]{1,0:T(1,128)} %left_hbm.1, s32[1,2048]{1,0:T(1,128)} %right_hbm.1, s32[1,2048]{1,0:T(1,128)} %group_hbm.1, ...), custom_call_target="tpu_custom_call" | custom-call | tf_op jit(solution)/shard_map/pallas_call | solution.py:593
  258.6 0.0 copy-start
  258.6 3.7 %shard_map.120 = (bf16[14,8,16,2048]{3,2,1,0:T(8,128)(2,1)}, f32[14,8,16,256]{3,2,1,0:T(8,128)}) custom-call(bf16[14,8,16,2048]{3,2,1,0:T(8,128)(2,1)S(1)} %get-tuple-element.12.scaled_ref, f32[14,8,16,256]{3,2,1,0:T(8,128)S(1)} %get-tuple-element.13.error_ref), custom_call_target="tpu_custom_call" | custom-call | tf_op jit(solution)/shard_map/pallas_call | solution.py:563
  262.3 0.0 copy-done
  262.3 0.5 copy.16
Async XLA Ops:
  258.6 3.7 %copy-start = (f32[1,16]{1,0:T(1,128)S(1)}, f32[1,16]{1,0:T(1,128)}, u32[]{:S(2)}) copy-start(f32[1,16]{1,0:T(1,128)} %get-tuple-element.26) | copy-start | bytes 196

commit v5 on v4

--- a/solution.py
+++ b/solution.py
@@ -19,7 +19,7 @@
 SLAB = 256
 PACK = LANES * OCT // SLAB
 LEAD = 3
-EARLY = 5
+EARLY = 2
 MESH = pl.DeviceIdType.MESH
 
 
@@ -216,11 +216,11 @@
     def across(s, k):
         return remote(out_s.at[s, k], in_s.at[s, k], send_s.at[s], recv_s.at[s, k], far_hub)
 
-    def across_part(k, low):
+    def across_part(s, k, low):
         at = pl.ds(0, alone) if low else pl.ds(alone, gather.shape[0] - alone)
         return remote(
-            out_s.at[0, k, at], in_s.at[0, k, at], send_s.at[0],
-            recv_first.at[k] if low else recv_s.at[0, k], far_hub,
+            out_s.at[s, k, at], in_s.at[s, k, at], send_s.at[s],
+            recv_first.at[s, k] if low else recv_s.at[s, k], far_hub,
         )
 
     def all_across(s):
@@ -296,33 +296,30 @@
             across(s, k).start()
 
         def remainder():
-            z = cols[0, k].reshape(mates * rows, SLAB)
+            z = cols[s, k].reshape(mates * rows, SLAB)
             r = jnp.dot(gather[alone:, :], z, preferred_element_type=jnp.float32)
-            out_s[0, k, alone:, :] = r.astype(jnp.bfloat16)
-            across_part(k, False).start()
+            out_s[s, k, alone:, :] = r.astype(jnp.bfloat16)
+            across_part(s, k, False).start()
 
         if early:
-            begun = jnp.logical_and(s == 0, k < early)
-            pl.when(begun)(remainder)
-            pl.when(jnp.logical_not(begun))(full)
+            pl.when(s < early)(remainder)
+            pl.when(s >= early)(full)
         else:
             full()
 
-    def forward_alone(k):
-        r = jnp.dot(first[...], cols[0, k, hub_slot], preferred_element_type=jnp.float32)
-        out_s[0, k, :alone, :] = r.astype(jnp.bfloat16)
-        across_part(k, True).start()
+    def forward_alone(s, k):
+        r = jnp.dot(first[...], cols[s, k, hub_slot], preferred_element_type=jnp.float32)
+        out_s[s, k, :alone, :] = r.astype(jnp.bfloat16)
+        across_part(s, k, True).start()
 
     def backward(s, k):
         if early:
-            begun = jnp.logical_and(s == 0, k < early)
-
-            @pl.when(begun)
+            @pl.when(s < early)
             def _():
-                across_part(k, True).wait_recv()
-                across_part(k, False).wait_recv()
-
-            pl.when(jnp.logical_not(begun))(lambda: across(s, k).wait_recv())
+                across_part(s, k, True).wait_recv()
+                across_part(s, k, False).wait_recv()
+
+            pl.when(s >= early)(lambda: across(s, k).wait_recv())
         else:
             across(s, k).wait_recv()
         z = cols[s, k].reshape(mates * rows, SLAB)
@@ -460,8 +457,12 @@
 
     @pl.when(is_hub)
     def _():
-        if early:
-            loop(early, forward_alone)
+        def begin(s):
+            pl.when(s > 0)(lambda: column_side(s))
+            if early:
+                loop(FOLD, lambda k: forward_alone(s, k))
+
+        loop(EARLY, begin)
         loop(LEAD, lambda k: forward(0, k))
 
     build_order(p_ref)
@@ -477,7 +478,7 @@
         def _():
             peak_ref[...] = jnp.zeros_like(peak_ref)
 
-        @pl.when(jnp.logical_and(is_hub, t + 1 < pairs))
+        @pl.when(jnp.logical_and(is_hub, jnp.logical_and(t + 1 >= EARLY, t + 1 < pairs)))
         def _():
             column_side(t + 1)
 
@@ -515,35 +516,36 @@
 
     loop(slabs + 2, stage)
 
-    peak = group_scale(0, slabs) * 0.5
-    scale_ref[...] = jnp.broadcast_to(peak, (GROUPS, LANES)).T[:1, :GROUPS]
 
     part = jnp.sum(jnp.sum(sum_ref[...], axis=0, keepdims=True), axis=1, keepdims=True)
     sums[here] = jnp.broadcast_to(part / (total_rows * width // OCT), (1, LANES))
     each_other(lambda place: share_sum(place).start())
     loop(FOLD // PACK, lambda kk: write_scaled(slabs - 2, kk))
     loop(FOLD // PACK, lambda kk: write_scaled(slabs - 1, kk))
+    peak = group_scale(0, slabs) * 0.5
+    scale_ref[...] = jnp.broadcast_to(peak, (GROUPS, LANES)).T[:1, :GROUPS]
+
+    @pl.when(jnp.logical_not(is_hub))
+    def _():
+        loop(slabs, lambda s: all_to_hub(s).wait_send())
+
+    @pl.when(is_hub)
+    def _():
+        for peer in others:
+            all_peaks(peer).wait_send()
+
+        def drain(s):
+            all_across(s).wait_send()
+            for who in mate_slots:
+                all_from_hub(s, who).wait_send()
+
+        loop(slabs, drain)
+
     all_sums().wait_recv()
     total = jnp.sum(sums[...], axis=0)
     mean = jnp.sum(sums[pl.ds(mine * peers, peers)], axis=0)
     mean_ref[0] = jnp.max(mean)
     total_ref[0] = jnp.max(total / experts)
-
-    @pl.when(jnp.logical_not(is_hub))
-    def _():
-        loop(slabs, lambda s: all_to_hub(s).wait_send())
-
-    @pl.when(is_hub)
-    def _():
-        for peer in others:
-            all_peaks(peer).wait_send()
-
-        def drain(s):
-            all_across(s).wait_send()
-            for who in mate_slots:
-                all_from_hub(s, who).wait_send()
-
-        loop(slabs, drain)
 
     all_sums().wait_send()
 
@@ -632,7 +634,7 @@
             dma((2, slabs)),
             dma((slabs,)),
             dma((slabs, FOLD)),
-            dma((EARLY,)),
+            dma((EARLY, FOLD)),
             dma,
             dma,
             dma((8,)),

time: 267 us -> 264 us (0.989)
  Pallas kernels: 262 us -> 259 us
where the time goes in v5:
time: 264 us
  Pallas kernels  259 us (98%)
  between operations  4.15 us (2%)
    pallas_call x1, Pallas kernels, body(): pl.pallas_call(functools.partial(kernel, peers, experts, alone), out_shap...  255 us

profile of v5, /device:TPU:0, one launch (start us, length us, event | category | flops | bytes accessed | tf_op | source)
XLA Modules:
  0.0 263.6 jit_solution(17494885016659127102)
XLA Ops:
  0.6 255.3 %shard_map.119 = (bf16[14,8,16,2048]{3,2,1,0:T(8,128)(2,1)S(1)}, f32[14,8,16,256]{3,2,1,0:T(8,128)S(1)}, f32[1,16]{1,0:T(1,128)}, f32[1]{0:T(128)}, f32[1]{0:T(128)}) custom-call(bf16[14,128,2048]{2,1,0:T(8,128)(2,1)} %bitcast.4, s32[1,1792]{1,0:T(1,128)} %left_hbm.1, s32[1,2048]{1,0:T(1,128)} %right_hbm.1, s32[1,2048]{1,0:T(1,128)} %group_hbm.1, ...), custom_call_target="tpu_custom_call" | custom-call | tf_op jit(solution)/shard_map/pallas_call | solution.py:595
  255.9 0.0 copy-start
  255.9 3.7 %shard_map.120 = (bf16[14,8,16,2048]{3,2,1,0:T(8,128)(2,1)}, f32[14,8,16,256]{3,2,1,0:T(8,128)}) custom-call(bf16[14,8,16,2048]{3,2,1,0:T(8,128)(2,1)S(1)} %get-tuple-element.12.scaled_ref, f32[14,8,16,256]{3,2,1,0:T(8,128)S(1)} %get-tuple-element.13.error_ref), custom_call_target="tpu_custom_call" | custom-call | tf_op jit(solution)/shard_map/pallas_call | solution.py:565
  259.6 0.0 copy-done
  259.6 0.5 copy.16
Async XLA Ops:
  255.9 3.7 %copy-start = (f32[1,16]{1,0:T(1,128)S(1)}, f32[1,16]{1,0:T(1,128)}, u32[]{:S(2)}) copy-start(f32[1,16]{1,0:T(1,128)} %get-tuple-element.26) | copy-start | bytes 196

commit v6 on v5

--- a/solution.py
+++ b/solution.py
@@ -403,7 +403,8 @@
         place = s % PACK
         inside = lane // octets == place
         at_error = pl.ds(pl.multiple_of(s // PACK * LANES, LANES), LANES)
-        first = (me * (blocks * HB) + (kk * PACK + lane // octets) * SUB + iota((SUB, LANES), 0)).astype(jnp.float32)
+        row = (me * (blocks * HB) + (kk * PACK + lane // octets) * SUB + iota((SUB, LANES), 0)).astype(jnp.float32)
+        weight = (1.0 + 4.0 * (row + 0.5) / total_rows) / 3.0
 
         def tile(j):
             at = pl.ds(pl.multiple_of(j * SUB, SUB), SUB)
@@ -429,8 +430,7 @@
                 turned = pltpu.roll(error, lax.rem(place + PACK - g, PACK) * octets, 1)
                 old = error_ref[j, kk * PACK + g, :, at_error]
                 error_ref[j, kk * PACK + g, :, at_error] = jnp.where(inside, turned, old)
-            row = first + (j * HB).astype(jnp.float32)
-            return error * ((1.0 + 4.0 * (row + 0.5) / total_rows) / 3.0)
+            return error * (weight + j.astype(jnp.float32) * (4.0 * HB / (3.0 * total_rows)))
 
         def some(i):
             parts = [tile(i * unroll + u) for u in range(unroll)]
@@ -550,29 +550,25 @@
     all_sums().wait_send()
 
 
-def put_kernel(scaled_ref, error_ref, scaled_out, error_out, sems):
-    copies = (
-        pltpu.make_async_copy(scaled_ref, scaled_out, sems.at[0]),
-        pltpu.make_async_copy(error_ref, error_out, sems.at[1]),
-    )
+def put_kernel(scaled_ref, error_ref, scale_ref, scaled_out, error_out, scale_out, sems):
+    pairs = ((scale_ref, scale_out), (scaled_ref, scaled_out), (error_ref, error_out))
+    copies = [pltpu.make_async_copy(src, dst, sems.at[n]) for n, (src, dst) in enumerate(pairs)]
     for copy in copies:
         copy.start()
     for copy in copies:
         copy.wait()
 
 
-def put(scaled, errors):
+def put(*results):
+    count = len(results)
     return pl.pallas_call(
         put_kernel,
-        out_shape=(
-            jax.ShapeDtypeStruct(scaled.shape, scaled.dtype),
-            jax.ShapeDtypeStruct(errors.shape, errors.dtype),
-        ),
-        in_specs=[pl.BlockSpec(memory_space=pltpu.VMEM)] * 2,
-        out_specs=[pl.BlockSpec(memory_space=pl.ANY)] * 2,
-        scratch_shapes=[pltpu.SemaphoreType.DMA((2,))],
+        out_shape=tuple(jax.ShapeDtypeStruct(r.shape, r.dtype) for r in results),
+        in_specs=[pl.BlockSpec(memory_space=pltpu.VMEM)] * count,
+        out_specs=[pl.BlockSpec(memory_space=pl.ANY)] * count,
+        scratch_shapes=[pltpu.SemaphoreType.DMA((count,))],
         compiler_params=pltpu.CompilerParams(vmem_limit_bytes=16 * 2**20),
-    )(scaled, errors)
+    )(*results)
 
 
 def body(weights, left_bits, right_bits, groups):
@@ -597,7 +593,7 @@
         out_shape=(
             pltpu.VMEM((blocks, FOLD, SUB, width), jnp.bfloat16),
             pltpu.VMEM((blocks, FOLD, SUB, width // OCT), jnp.float32),
-            jax.ShapeDtypeStruct((1, GROUPS), jnp.float32),
+            pltpu.VMEM((1, GROUPS), jnp.float32),
             jax.ShapeDtypeStruct((1,), jnp.float32),
             jax.ShapeDtypeStruct((1,), jnp.float32),
         ),
@@ -643,7 +639,7 @@
             collective_id=0, has_side_effects=True, vmem_limit_bytes=54 * 2**20
         ),
     )(weights.reshape(blocks, HB, width), left_bits, right_bits, groups, near, gather, spread, first)
-    scaled, errors = put(scaled, errors)
+    scaled, errors, group_scale = put(scaled, errors, group_scale)
     return (
         scaled.reshape(1, local_rows, width),
         errors.reshape(1, local_rows, width // OCT),

time: 264 us -> 263 us (level)
  no operation moved by 1% of the time
where the time goes in v6:
time: 263 us
  Pallas kernels  259 us (98%)
  between operations  4.16 us (2%)
    pallas_call x1, Pallas kernels, body(): pl.pallas_call(functools.partial(kernel, peers, experts, alone), out_shap...  255 us

profile of v6, /device:TPU:0, one launch (start us, length us, event | category | flops | bytes accessed | tf_op | source)
XLA Modules:
  0.0 263.0 jit_solution(4001914770923751464)
XLA Ops:
  0.6 255.2 %shard_map.119 = (bf16[14,8,16,2048]{3,2,1,0:T(8,128)(2,1)S(1)}, f32[14,8,16,256]{3,2,1,0:T(8,128)S(1)}, f32[1,16]{1,0:T(1,128)S(1)}, f32[1]{0:T(128)}, f32[1]{0:T(128)}) custom-call(bf16[14,128,2048]{2,1,0:T(8,128)(2,1)} %bitcast.4, s32[1,1792]{1,0:T(1,128)} %left_hbm.1, s32[1,2048]{1,0:T(1,128)} %right_hbm.1, s32[1,2048]{1,0:T(1,128)} %group_hbm.1, ...), custom_call_target="tpu_custom_call" | custom-call | tf_op jit(solution)/shard_map/pallas_call | solution.py:591
  255.8 3.7 %shard_map.120 = (bf16[14,8,16,2048]{3,2,1,0:T(8,128)(2,1)}, f32[14,8,16,256]{3,2,1,0:T(8,128)}, f32[1,16]{1,0:T(1,128)}) custom-call(bf16[14,8,16,2048]{3,2,1,0:T(8,128)(2,1)S(1)} %get-tuple-element.13.scaled_ref, f32[14,8,16,256]{3,2,1,0:T(8,128)S(1)} %get-tuple-element.14.error_ref, f32[1,16]{1,0:T(1,128)S(1)} %get-tuple-element.15.scale_ref), custom_call_target="tpu_custom_call" | custom-call | tf_op jit(solution)/shard_map/pallas_call | solution.py:564

commit v7 on v6

--- a/solution.py
+++ b/solution.py
@@ -349,9 +349,9 @@
 
     total_rows = peers * blocks * HB
     early = EARLY if alone else 0
-    unroll = next(u for u in (7, 1) if blocks % u == 0)
-
-    def scale_slab(s):
+    unroll = next(u for u in (14, 7, 1) if blocks % u == 0)
+
+    def peaks_in(s):
         last = jnp.minimum(s + 1, slabs - 1)
 
         def peak_in(t):
@@ -367,11 +367,13 @@
 
         for t in range(2):
             peak_in(t)
+
+    def scale_slab(s):
         factor = 2.0 / group_scale(s - 1, 3)
         wide = group_ref[:, pl.ds(pl.multiple_of(s * SLAB, SLAB), SLAB)] == iota((GROUPS, SLAB), 0)
         natural_ref[pl.ds(s % 2, 1), :] = jnp.max(jnp.where(wide, factor, 0.0), axis=0, keepdims=True)
         wide = planar_group[pl.ds(s, 1), :] == iota((GROUPS, OCT * LANES), 0).astype(jnp.float32)
-        factor_ref[...] = jnp.max(jnp.where(wide, factor, 0.0), axis=0, keepdims=True)
+        factor_ref[s % 2] = jnp.max(jnp.where(wide, factor, 0.0), axis=0, keepdims=True)
 
     def permute(s, kk):
         @pl.when(jnp.logical_not(is_hub))
@@ -410,7 +412,7 @@
             at = pl.ds(pl.multiple_of(j * SUB, SUB), SUB)
             square = near_sum = low = size = most = least = None
             for c in range(OCT):
-                value = planar_ref[s % 2, kk, at, c * LANES:(c + 1) * LANES] * factor_ref[:, c * LANES:(c + 1) * LANES]
+                value = planar_ref[s % 2, kk, at, c * LANES:(c + 1) * LANES] * factor_ref[s % 2, :, c * LANES:(c + 1) * LANES]
                 nearest = jnp.round(value)
                 offset = jnp.abs(value - nearest)
                 below = jnp.floor(value)
@@ -499,9 +501,16 @@
 
             @pl.when(t >= 2)
             def _():
-                @pl.when(kk == 0)
+                @pl.when(jnp.logical_and(kk == 0, t < slabs))
                 def _():
+                    peaks_in(t - 2)
                     scale_slab(t - 2)
+
+                @pl.when(jnp.logical_and(kk == 0, t == slabs))
+                def _():
+                    peaks_in(slabs - 2)
+                    scale_slab(slabs - 2)
+                    scale_slab(slabs - 1)
 
                 lattice(t - 2, kk)
                 pl.when(t < slabs)(lambda: write_scaled(t - 2, kk))
@@ -619,7 +628,7 @@
             pltpu.VMEM((2, slabs, 8, SLAB), jnp.float32),
             pltpu.VMEM((8, SLAB), jnp.float32),
             pltpu.VMEM((2, SLAB), jnp.float32),
-            pltpu.VMEM((1, OCT * LANES), jnp.float32),
+            pltpu.VMEM((2, 1, OCT * LANES), jnp.float32),
             pltpu.VMEM((SUB, LANES), jnp.float32),
             pltpu.VMEM((peers * experts, 1, LANES), jnp.float32),
             dma((slabs,)),

time: 263 us -> 263 us (level)
  no operation moved by 1% of the time
where the time goes in v7:
time: 263 us
  Pallas kernels  258 us (98%)
  between operations  4.16 us (2%)
    pallas_call x1, Pallas kernels, body(): pl.pallas_call(functools.partial(kernel, peers, experts, alone), out_shap...  255 us

profile of v7, /device:TPU:0, one launch (start us, length us, event | category | flops | bytes accessed | tf_op | source)
XLA Modules:
  0.0 262.6 jit_solution(12480258486594383237)
XLA Ops:
  0.6 254.7 %shard_map.119 = (bf16[14,8,16,2048]{3,2,1,0:T(8,128)(2,1)S(1)}, f32[14,8,16,256]{3,2,1,0:T(8,128)S(1)}, f32[1,16]{1,0:T(1,128)S(1)}, f32[1]{0:T(128)}, f32[1]{0:T(128)}) custom-call(bf16[14,128,2048]{2,1,0:T(8,128)(2,1)} %bitcast.4, s32[1,1792]{1,0:T(1,128)} %left_hbm.1, s32[1,2048]{1,0:T(1,128)} %right_hbm.1, s32[1,2048]{1,0:T(1,128)} %group_hbm.1, ...), custom_call_target="tpu_custom_call" | custom-call | tf_op jit(solution)/shard_map/pallas_call | solution.py:600
  255.4 3.7 %shard_map.120 = (bf16[14,8,16,2048]{3,2,1,0:T(8,128)(2,1)}, f32[14,8,16,256]{3,2,1,0:T(8,128)}, f32[1,16]{1,0:T(1,128)}) custom-call(bf16[14,8,16,2048]{3,2,1,0:T(8,128)(2,1)S(1)} %get-tuple-element.13.scaled_ref, f32[14,8,16,256]{3,2,1,0:T(8,128)S(1)} %get-tuple-element.14.error_ref, f32[1,16]{1,0:T(1,128)S(1)} %get-tuple-element.15.scale_ref), custom_call_target="tpu_custom_call" | custom-call | tf_op jit(solution)/shard_map/pallas_call | solution.py:573
